TPU v7x, 512 devices: a whole 4x8x8 slice. The times are simulated.
512 devices in a mesh: atoms: 128 (over z, x_lo, y), waves: 4 (over x_hi, core).
Axes of the slice: x: 4 (x_hi: 2, x_lo: 2; x = x_hi * 2 + x_lo), y: 8, z: 8, core: 2. Of those that a mesh axis runs over, the one named last changes fastest.
Arguments:
- features: bfloat16 [32768, 512], P('atoms'), may hold values from -6 to 6
- positions: int32 [3, 32768], P(None, 'atoms'), may hold values from 0 to 65535
- neighbours: int32 [256, 12], P('atoms'), may hold values from 0 to 255, as said below
- wavevectors: int32 [3, 4096], P(None, 'waves'), may hold values from -16 to 16
- radial_width: float32 [8], P('waves'), may hold values from 0.05 to 0.3
- short_weight: bfloat16 [8, 512, 512], P('waves'), may hold values from -0.09375 to 0.09375
- latent_weight: bfloat16 [512, 256], replicated, may hold values from -0.25 to 0.25
- mix_weight: float32 [256, 256], replicated, may hold values from -0.375 to 0.375
- filter_rate: float32 [256], replicated, may hold values from 0.0005 to 0.02
- out_weight: bfloat16 [256, 512], replicated, may hold values from -0.375 to 0.375
Outputs:
- message: bfloat16 [32768, 512], P('atoms', 'waves')
Inputs may be any that keep to these rules, and one draw needn't show every extreme that they name: `neighbours`: row b holds 12 different block numbers, each within 7 blocks of b counted cyclically over the 256 blocks; b itself may appear.
All inputs are finite; a program needn't handle non-finite values.
Results may differ from a plain program's by a relative error of at most 0.012.
Values may be sent and summed in bfloat16 or wider, within the bound.
No kernel may reach another device: no remote copies, remote signals or barrier semaphores. Data moves between devices by JAX's collectives and lax.ppermute only.
A program may use at most 64 MiB of HBM per device.

v0:
```python
import math

import jax
import jax.numpy as jnp
from jax import lax
from jax.sharding import Mesh
from jax.sharding import PartitionSpec as P

K = 4096
RADIAL = 8
BLOCK = 128
NBR = 12
REACH = 7
ATOMS = ("atoms_0", "atoms_1", "atoms_2")


cutoff = 0.5


def shifted(value, axis, steps):
    count = lax.axis_size(axis)
    pairs = [(source, (source + steps) % count) for source in range(count)]
    return lax.ppermute(value, axis, pairs)


def in_blocks(value, dim, count):
    before, after = (value.shape[:dim], value.shape[dim + 1 :])
    return jnp.moveaxis(value.reshape(*before, count, -1, *after), dim, 0)


def sum_at_owner(value, axis, dim):
    pieces = in_blocks(value, dim, lax.axis_size(axis))
    arrived = lax.all_to_all(pieces, axis, split_axis=0, concat_axis=0, tiled=True)
    return arrived.sum(axis=0)


def summed_rows(value, axes, dim):
    far, near = axes
    pieces = in_blocks(value, dim, lax.axis_size(far))
    nearer = sum_at_owner(pieces, near, dim + 1)
    arrived = lax.all_to_all(nearer, far, split_axis=0, concat_axis=0, tiled=True)
    return arrived.sum(axis=0)


def padded_to(lines, count):
    spare = -lines.shape[0] % count
    if not spare:
        return lines
    return jnp.concatenate([lines, jnp.zeros((spare, *lines.shape[1:]), lines.dtype)])


def copy_for_each(value, axis):
    copies = jnp.broadcast_to(value, (lax.axis_size(axis), *value.shape))
    return lax.all_to_all(copies, axis, split_axis=0, concat_axis=0, tiled=True)


def in_order(pieces, dim):
    pieces = jnp.moveaxis(pieces, 0, dim)
    lengths = pieces.shape
    return pieces.reshape(*lengths[:dim], lengths[dim] * lengths[dim + 1], *lengths[dim + 2 :])


def gather_axes(value, axes, dim):
    far, near = axes
    pieces = copy_for_each(copy_for_each(value, far), near)
    return in_order(pieces.swapaxes(0, 1).reshape(-1, *value.shape), dim)


def sum_by_parts(value, axes):
    lines = value.reshape(-1, value.shape[-1])
    own = summed_rows(padded_to(lines, lax.axis_size(axes[0]) * lax.axis_size(axes[1])), axes, 0)
    whole = gather_axes(own, axes, 0)
    return whole[: len(lines)].reshape(value.shape)


def sent_and_summed(value, axis, dim):
    count = lax.axis_size(axis)
    pieces = lax.all_to_all(in_blocks(value, dim, count), axis, 0, 0, tiled=True)
    return jnp.sum(pieces.astype(jnp.float32), axis=0)


def kernels(own_pos, near_pos, centers, radial_width):
    offsets = own_pos[:, None, :, None] - near_pos[:, :, None, :]
    offsets = jnp.mod(offsets, 65536)
    offsets = jnp.where(offsets >= 32768, offsets - 65536, offsets)
    coords = offsets.astype(jnp.float32) * (1.0 / 65536.0)
    dist_sq = jnp.sum(coords * coords, axis=0)
    distance = jnp.sqrt(dist_sq)
    smooth = jnp.where(
        dist_sq < cutoff * cutoff, jnp.square(1.0 - dist_sq / (cutoff * cutoff)), 0.0
    )
    shaped = (distance[None] - centers[:, None, None, None]) / radial_width[:, None, None, None]
    norm_scale = 1.0 / math.sqrt(NBR * BLOCK)
    return (jnp.exp(-jnp.square(shaped)) * smooth[None] * norm_scale).astype(jnp.bfloat16)


def phases_of(wavevectors, spots):
    phase_turn = (
        wavevectors[0][:, None] * spots[0][None, :]
        + wavevectors[1][:, None] * spots[1][None, :]
        + wavevectors[2][:, None] * spots[2][None, :]
    )
    phase_turn = jnp.mod(phase_turn, 65536)
    angles = phase_turn.astype(jnp.float32) * (2.0 * math.pi / 65536.0)
    return jnp.concatenate([jnp.cos(angles), jnp.sin(angles)], axis=0).astype(jnp.bfloat16)


def filter_gain(wavevectors, filter_rate):
    lengths = jnp.sum(wavevectors * wavevectors, axis=0).astype(jnp.float32)
    return jnp.exp(-lengths[:, None] * filter_rate[None, :])


def local(
    features,
    positions,
    neighbours,
    wavevectors,
    radial_width,
    short_weight,
    latent_weight,
    mix_weight,
    filter_rate,
    out_weight,
):
    row_count = features.shape[0]
    channels = features.shape[1]
    blocks_here = row_count // BLOCK
    atom_devices = lax.axis_size(ATOMS)
    total_blocks = blocks_here * atom_devices
    reach_hops = -(-REACH // blocks_here)
    window_feat = []
    window_pos = []
    for offset in range(-reach_hops, reach_hops + 1):
        if offset == 0:
            arrived = (features, positions)
        else:
            arrived = shifted((features, positions), ATOMS, -offset)
        window_feat.append(arrived[0])
        window_pos.append(arrived[1])
    window_feat = jnp.concatenate(window_feat, axis=0).reshape(-1, BLOCK, channels)
    window_pos = jnp.concatenate(window_pos, axis=1).reshape(3, -1, BLOCK)
    first_block = lax.axis_index(ATOMS) * blocks_here - reach_hops * blocks_here
    local_near = jnp.mod(neighbours - first_block, total_blocks)
    own_pos = positions.reshape(3, blocks_here, BLOCK)
    local_kernels = radial_width.shape[0]
    kernel_ids = lax.axis_index("waves") * local_kernels + jnp.arange(
        local_kernels, dtype=jnp.int32
    )
    centers = cutoff * kernel_ids.astype(jnp.float32) / (RADIAL - 1)
    flat_weight = short_weight.reshape(local_kernels * channels, channels)

    def short_block(block_index):
        near_blocks = local_near[block_index]
        near_feat = window_feat[near_blocks]
        near_pos = window_pos[:, near_blocks]
        weights = kernels(own_pos[:, block_index], near_pos, centers, radial_width)
        gathered = jnp.einsum(
            "rjia,jac->irc", weights, near_feat, preferred_element_type=jnp.float32
        )
        gathered = gathered.astype(jnp.bfloat16).reshape(BLOCK, local_kernels * channels)
        return jnp.dot(gathered, flat_weight, preferred_element_type=jnp.float32)

    short_range = lax.map(short_block, jnp.arange(blocks_here, dtype=jnp.int32)).reshape(
        row_count, channels
    )
    latent = jnp.dot(features, latent_weight, preferred_element_type=jnp.float32).astype(
        jnp.bfloat16
    )
    phases = phases_of(wavevectors, positions)
    partial_factors = jnp.dot(phases, latent, preferred_element_type=jnp.float32)
    gain = filter_gain(wavevectors, filter_rate)
    gain = jnp.concatenate([gain, gain], axis=0)
    norm_scale = 1.0 / math.sqrt(row_count * atom_devices)
    factors = sum_by_parts(partial_factors, ("atoms_0", ("atoms_1", "atoms_2")))
    mixed = jnp.dot(factors, mix_weight, precision=lax.Precision.HIGHEST)
    filtered = (gain * mixed * norm_scale).astype(jnp.bfloat16)
    summed = lax.dot_general(
        phases, filtered, (((0,), (0,)), ((), ())), preferred_element_type=jnp.float32
    )
    summed = (summed * (1.0 / math.sqrt(K))).astype(jnp.bfloat16)
    long_range = jnp.dot(summed, out_weight, preferred_element_type=jnp.float32)
    combined = sent_and_summed((short_range + long_range).astype(jnp.bfloat16), "waves", 1)
    return combined.astype(jnp.bfloat16)


def solution(mesh):
    torus = Mesh(
        mesh.devices.reshape(8, 2, 8, mesh.shape["waves"]),
        ("atoms_0", "atoms_1", "atoms_2", "waves"),
    )
    placed = (
        P(ATOMS, None),
        P(None, ATOMS),
        P(ATOMS, None),
        P(None, "waves"),
        P("waves"),
        P("waves", None, None),
        P(),
        P(),
        P(),
        P(),
    )
    return jax.shard_map(
        local, mesh=torus, in_specs=placed, out_specs=P(ATOMS, "waves"), check_vma=False
    )
```

profile of v0, /device:TPU:1, one launch (start us, length us, event | category | flops | bytes accessed | tf_op | source)
XLA Modules:
  0.0 307.8 jit_solution(10832301400895146922)
XLA Ops:
  1.6 4.8 %cosine_convert_fusion = (bf16[1024,256]{1,0:T(8,128)(2,1)S(1)}, bf16[1024,256]{1,0:T(8,128)(2,1)S(1)}) fusion(s32[256]{0:T(256)S(1)} %bitcast.100, s32[1024]{0:T(1024)S(1)} %bitcast.98, s32[256]{0:T(256)S(1)} %bitcast.101, s32[1024]{0:T(1024)S(1)} %bitcast.97, s32[256]{0:T(256)S(1)} %bitcast.99, s32[1024]{0:T(1024)S(1)} %bitcast.96), kind=kLoop, calls=%fused_computation.55 | loop fusion | flops 5242880 | bytes 1063936 | tf_op jit(solution)/shard_map/convert.1
  9.9 8.8 %all-to-all-start = ((f32[16,8,16,256]{3,2,1,0:T(8,128)}), f32[16,8,16,256]{3,2,1,0:T(8,128)S(1)}, u32[]{:S(2)}, u32[]{:S(2)}) async-start(f32[16,8,16,256]{3,2,1,0:T(8,128)} %bitcast.89), calls=%async_computation | async-start | bytes 4194304 | tf_op jit(solution)/shard_map/all_to_all | solution.py:33
  18.8 7.2 %collective-permute-start = (bf16[256,512]{1,0:T(8,128)(2,1)S(1)}, bf16[256,512]{1,0:T(8,128)(2,1)}, u32[]{:S(2)}, u32[]{:S(2)}) collective-permute-start(bf16[256,512]{1,0:T(8,128)(2,1)S(1)} %copy-done.5), channel_id=1, source_target_pairs={{0,16},{4,20},{8,24},{12,28},{16,32},{20,36},{24,40},{28,44},{32,4... | collective-permute-start | bytes 786440 | tf_op jit(solution)/shard_map/ppermute | solution.py:23
  25.9 2.2 collective-permute-start.1
  28.1 4.0 %collective-permute-start.2 = (bf16[256,512]{1,0:T(8,128)(2,1)S(1)}, bf16[256,512]{1,0:T(8,128)(2,1)}, u32[]{:S(2)}, u32[]{:S(2)}) collective-permute-start(bf16[256,512]{1,0:T(8,128)(2,1)S(1)} %copy-done.5), channel_id=1, source_target_pairs={{0,8},{4,12},{8,16},{12,20},{16,24},{20,28},{24,32},{28,36},{32,40... | collective-permute-start | bytes 786440 | tf_op jit(solution)/shard_map/ppermute | solution.py:23
  32.1 3.1 %collective-permute-start.3 = (bf16[256,512]{1,0:T(8,128)(2,1)S(1)}, bf16[256,512]{1,0:T(8,128)(2,1)S(1)}, u32[]{:S(2)}, u32[]{:S(2)}) collective-permute-start(bf16[256,512]{1,0:T(8,128)(2,1)S(1)} %copy-done.5), channel_id=1, source_target_pairs={{0,4},{4,8},{8,12},{12,16},{16,20},{20,24},{24,28},{28,32},{32,36}... | collective-permute-start | bytes 786440 | tf_op jit(solution)/shard_map/ppermute | solution.py:23
  35.3 5.2 %collective-permute-start.8 = (s32[3,256]{1,0:T(4,128)S(1)}, s32[3,256]{1,0:T(4,128)S(1)}, u32[]{:S(2)}, u32[]{:S(2)}) collective-permute-start(s32[3,256]{1,0:T(4,128)S(1)} %copy-done.7), channel_id=1, source_target_pairs={{0,16},{4,20},{8,24},{12,28},{16,32},{20,36},{24,40},{28,44},{32,4... | collective-permute-start | bytes 9224 | tf_op jit(solution)/shard_map/ppermute | solution.py:23
  41.8 81.6 %collective-permute-done.8 = s32[3,256]{1,0:T(4,128)S(1)} collective-permute-done((s32[3,256]{1,0:T(4,128)S(1)}, s32[3,256]{1,0:T(4,128)S(1)}, u32[]{:S(2)}, u32[]{:S(2)}) %collective-permute-start.8) | collective-permute-done | bytes 3104 | tf_op jit(solution)/shard_map/ppermute | solution.py:23
  123.3 1.9 collective-permute-start.9
  125.2 8.4 %collective-permute-done.9 = s32[3,256]{1,0:T(4,128)S(1)} collective-permute-done((s32[3,256]{1,0:T(4,128)S(1)}, s32[3,256]{1,0:T(4,128)S(1)}, u32[]{:S(2)}, u32[]{:S(2)}) %collective-permute-start.9) | collective-permute-done | bytes 3104 | tf_op jit(solution)/shard_map/ppermute | solution.py:23
  133.7 2.4 collective-permute-start.10
  136.1 7.0 %collective-permute-done.10 = s32[3,256]{1,0:T(4,128)S(1)} collective-permute-done((s32[3,256]{1,0:T(4,128)S(1)}, s32[3,256]{1,0:T(4,128)S(1)}, u32[]{:S(2)}, u32[]{:S(2)}) %collective-permute-start.10) | collective-permute-done | bytes 3104 | tf_op jit(solution)/shard_map/ppermute | solution.py:23
  145.1 6.6 %collective-permute-done.11 = s32[3,256]{1,0:T(4,128)S(1)} collective-permute-done((s32[3,256]{1,0:T(4,128)S(1)}, s32[3,256]{1,0:T(4,128)S(1)}, u32[]{:S(2)}, u32[]{:S(2)}) %collective-permute-start.11) | collective-permute-done | bytes 3104 | tf_op jit(solution)/shard_map/ppermute | solution.py:23
  151.7 1.9 collective-permute-start.12
  153.6 2.7 collective-permute-done.12
  158.2 3.3 %collective-permute-done.13 = s32[3,256]{1,0:T(4,128)S(1)} collective-permute-done((s32[3,256]{1,0:T(4,128)S(1)}, s32[3,256]{1,0:T(4,128)S(1)}, u32[]{:S(2)}, u32[]{:S(2)}) %collective-permute-start.13) | collective-permute-done | bytes 3104 | tf_op jit(solution)/shard_map/ppermute | solution.py:23
  161.6 5.6 %collective-permute-start.14 = (s32[3,256]{1,0:T(4,128)S(1)}, s32[3,256]{1,0:T(4,128)S(1)}, u32[]{:S(2)}, u32[]{:S(2)}) collective-permute-start(s32[3,256]{1,0:T(4,128)S(1)} %copy-done.7), channel_id=1, source_target_pairs={{0,500},{4,504},{8,508},{12,0},{16,4},{20,8},{24,12},{28,16},{32,2... | collective-permute-start | bytes 9224 | tf_op jit(solution)/shard_map/ppermute | solution.py:23
  167.9 9.6 %collective-permute-start.15 = (s32[3,256]{1,0:T(4,128)S(1)}, s32[3,256]{1,0:T(4,128)S(1)}, u32[]{:S(2)}, u32[]{:S(2)}) collective-permute-start(s32[3,256]{1,0:T(4,128)S(1)} %copy-done.7), channel_id=1, source_target_pairs={{0,496},{4,500},{8,504},{12,508},{16,0},{20,4},{24,8},{28,12},{32,... | collective-permute-start | bytes 9224 | tf_op jit(solution)/shard_map/ppermute | solution.py:23
  178.2 15.1 %collective-permute-start.4 = (bf16[256,512]{1,0:T(8,128)(2,1)S(1)}, bf16[256,512]{1,0:T(8,128)(2,1)}, u32[]{:S(2)}, u32[]{:S(2)}) collective-permute-start(bf16[256,512]{1,0:T(8,128)(2,1)S(1)} %copy-done.5), channel_id=1, source_target_pairs={{0,508},{4,0},{8,4},{12,8},{16,12},{20,16},{24,20},{28,24},{32,28}... | collective-permute-start | bytes 786440 | tf_op jit(solution)/shard_map/ppermute | solution.py:23
  193.4 1.9 collective-permute-start.5
  197.0 1.9 collective-permute-start.6
  200.5 1.9 collective-permute-start.7
  204.9 3.4 %all-to-all-start.1 = ((f32[8,16,256]{2,1,0:T(8,128)}), f32[8,16,256]{2,1,0:T(8,128)S(1)}, u32[]{:S(2)}, u32[]{:S(2)}) async-start(f32[8,16,256]{2,1,0:T(8,128)} %reduce_sum.52), calls=%async_computation.1 | async-start | bytes 262144 | tf_op jit(solution)/shard_map/all_to_all | solution.py:41
  209.8 6.4 %all-to-all-done.1 = f32[8,16,256]{2,1,0:T(8,128)S(1)} async-done(((f32[8,16,256]{2,1,0:T(8,128)}), f32[8,16,256]{2,1,0:T(8,128)S(1)}, u32[]{:S(2)}, u32[]{:S(2)}) %all-to-all-start.1) | async-done | bytes 131104 | tf_op jit(solution)/shard_map/all_to_all | solution.py:41
  216.8 3.4 %all-to-all-start.2 = ((f32[8,16,256]{2,1,0:T(8,128)}), f32[8,16,256]{2,1,0:T(8,128)S(1)}, u32[]{:S(2)}, u32[]{:S(2)}) async-start(f32[8,16,256]{2,1,0:T(8,128)} %broadcast_in_dim.30), calls=%async_computation.2 | async-start | bytes 262144 | tf_op jit(solution)/shard_map/all_to_all | solution.py:54
  223.6 4.5 %all-to-all-done.2 = f32[8,16,256]{2,1,0:T(8,128)S(1)} async-done(((f32[8,16,256]{2,1,0:T(8,128)}), f32[8,16,256]{2,1,0:T(8,128)S(1)}, u32[]{:S(2)}, u32[]{:S(2)}) %all-to-all-start.2) | async-done | bytes 131104 | tf_op jit(solution)/shard_map/all_to_all | solution.py:54
  229.7 11.0 %all-to-all-start.3 = ((f32[16,8,16,256]{3,2,1,0:T(8,128)}), f32[16,8,16,256]{3,2,1,0:T(8,128)}, u32[]{:S(2)}, u32[]{:S(2)}) async-start(f32[16,8,16,256]{3,2,1,0:T(8,128)} %broadcast_in_dim.31), calls=%async_computation.3 | async-start | bytes 4194304 | tf_op jit(solution)/shard_map/all_to_all | solution.py:54
  244.1 18.6 %while.13 = (s32[]{:T(128)}, f32[2,128,512]{2,1,0:T(8,128)}, s32[2]{0:T(128)S(1)}, s32[2,12]{1,0:T(2,128)S(1)}, bf16[18,128,512]{2,1,0:T(8,128)(2,1)}, /*index=5...) while((s32[]{:T(128)}, f32[2,128,512]{2,1,0:T(8,128)}, ...), condition=%wide.region_2.3_spmd.clone, body=%wide.region_0.2_spmd.clone.sunk | while | flops 551748608 | bytes 11373515 | solution.py:163
  246.7 2.3 gather_fusion
  256.0 2.3 gather_fusion
  262.7 16.5 %all-to-all-done.3 = f32[16,8,16,256]{3,2,1,0:T(8,128)} async-done(((f32[16,8,16,256]{3,2,1,0:T(8,128)}), f32[16,8,16,256]{3,2,1,0:T(8,128)}, u32[]{:S(2)}, u32[]{:S(2)}) %all-to-all-start.3) | async-done | bytes 2097184 | tf_op jit(solution)/shard_map/all_to_all | solution.py:54
  284.8 22.4 %all_to_all.25 = bf16[4,256,128]{2,1,0:T(8,128)(2,1)S(1)} all-to-all(bf16[4,256,128]{2,1,0:T(8,128)(2,1)S(1)} %bitcast.93), channel_id=1, replica_groups=mesh['atoms_0'=8,'atoms_1'=2,'atoms_2'=8,'waves'=4] {'waves'}, dimensions={0} | all-to-all | bytes 524288 | tf_op jit(solution)/shard_map/all_to_all | solution.py:78
  (96 shorter events, 44.2 us)
Async XLA Ops:
  0.0 6.4 %copy-start = (bf16[512,256]{1,0:T(8,128)(2,1)S(1)}, bf16[512,256]{1,0:T(8,128)(2,1)}, u32[]{:S(2)}) copy-start(bf16[512,256]{1,0:T(8,128)(2,1)} %param.18) | copy-start | bytes 786436
  6.4 3.5 %copy-start.3 = (bf16[1024,256]{1,0:T(8,128)(2,1)}, bf16[1024,256]{1,0:T(8,128)(2,1)S(1)}, u32[]{:S(2)}) copy-start(bf16[1024,256]{1,0:T(8,128)(2,1)S(1)} %get-tuple-element.182) | copy-start | bytes 1572868
  9.9 8.9 %copy-start.5 = (bf16[256,512]{1,0:T(8,128)(2,1)S(1)}, bf16[256,512]{1,0:T(8,128)(2,1)}, u32[]{:S(2)}) copy-start(bf16[256,512]{1,0:T(8,128)(2,1)} %param.12) | copy-start | bytes 786436
  9.9 25.3 %copy-start.7 = (s32[3,256]{1,0:T(4,128)S(1)}, s32[3,256]{1,0:T(4,128)}, u32[]{:S(2)}) copy-start(s32[3,256]{1,0:T(4,128)} %param.13) | copy-start | bytes 9220
  9.9 30.6 %copy-start.8 = (s32[3,1024]{1,0:T(4,128)S(1)}, s32[3,1024]{1,0:T(4,128)}, u32[]{:S(2)}) copy-start(s32[3,1024]{1,0:T(4,128)} %param.15) | copy-start | bytes 36868
  9.9 30.6 %copy-start.9 = (f32[256]{0:T(256)S(1)}, f32[256]{0:T(256)}, u32[]{:S(2)}) copy-start(f32[256]{0:T(256)} %param.20) | copy-start | bytes 3076
  9.9 31.8 %copy-start.10 = (s32[2,12]{1,0:T(2,128)S(1)}, s32[2,12]{1,0:T(2,128)}, u32[]{:S(2)}) copy-start(s32[2,12]{1,0:T(2,128)} %param.14) | copy-start | bytes 292
  9.9 194.2 %all-to-all-start = ((f32[16,8,16,256]{3,2,1,0:T(8,128)}), f32[16,8,16,256]{3,2,1,0:T(8,128)S(1)}, u32[]{:S(2)}, u32[]{:S(2)}) async-start(f32[16,8,16,256]{3,2,1,0:T(8,128)} %bitcast.89), calls=%async_computation | async-start | bytes 4194304 | tf_op jit(solution)/shard_map/all_to_all | solution.py:33
  18.8 174.6 %collective-permute-start = (bf16[256,512]{1,0:T(8,128)(2,1)S(1)}, bf16[256,512]{1,0:T(8,128)(2,1)}, u32[]{:S(2)}, u32[]{:S(2)}) collective-permute-start(bf16[256,512]{1,0:T(8,128)(2,1)S(1)} %copy-done.5), channel_id=1, source_target_pairs={{0,16},{4,20},{8,24},{12,28},{16,32},{20,36},{24,40},{28,44},{32,4... | collective-permute-start | bytes 786440 | tf_op jit(solution)/shard_map/ppermute | solution.py:23
  25.9 171.0 %collective-permute-start.1 = (bf16[256,512]{1,0:T(8,128)(2,1)S(1)}, bf16[256,512]{1,0:T(8,128)(2,1)}, u32[]{:S(2)}, u32[]{:S(2)}) collective-permute-start(bf16[256,512]{1,0:T(8,128)(2,1)S(1)} %copy-done.5), channel_id=1, source_target_pairs={{0,12},{4,16},{8,20},{12,24},{16,28},{20,32},{24,36},{28,40},{32,4... | collective-permute-start | bytes 786440 | tf_op jit(solution)/shard_map/ppermute | solution.py:23
  28.1 172.4 %collective-permute-start.2 = (bf16[256,512]{1,0:T(8,128)(2,1)S(1)}, bf16[256,512]{1,0:T(8,128)(2,1)}, u32[]{:S(2)}, u32[]{:S(2)}) collective-permute-start(bf16[256,512]{1,0:T(8,128)(2,1)S(1)} %copy-done.5), channel_id=1, source_target_pairs={{0,8},{4,12},{8,16},{12,20},{16,24},{20,28},{24,32},{28,36},{32,40... | collective-permute-start | bytes 786440 | tf_op jit(solution)/shard_map/ppermute | solution.py:23
  32.1 176.2 %collective-permute-start.3 = (bf16[256,512]{1,0:T(8,128)(2,1)S(1)}, bf16[256,512]{1,0:T(8,128)(2,1)S(1)}, u32[]{:S(2)}, u32[]{:S(2)}) collective-permute-start(bf16[256,512]{1,0:T(8,128)(2,1)S(1)} %copy-done.5), channel_id=1, source_target_pairs={{0,4},{4,8},{8,12},{12,16},{16,20},{20,24},{24,28},{28,32},{32,36}... | collective-permute-start | bytes 786440 | tf_op jit(solution)/shard_map/ppermute | solution.py:23
  35.3 88.1 %collective-permute-start.8 = (s32[3,256]{1,0:T(4,128)S(1)}, s32[3,256]{1,0:T(4,128)S(1)}, u32[]{:S(2)}, u32[]{:S(2)}) collective-permute-start(s32[3,256]{1,0:T(4,128)S(1)} %copy-done.7), channel_id=1, source_target_pairs={{0,16},{4,20},{8,24},{12,28},{16,32},{20,36},{24,40},{28,44},{32,4... | collective-permute-start | bytes 9224 | tf_op jit(solution)/shard_map/ppermute | solution.py:23
  123.3 10.4 %collective-permute-start.9 = (s32[3,256]{1,0:T(4,128)S(1)}, s32[3,256]{1,0:T(4,128)S(1)}, u32[]{:S(2)}, u32[]{:S(2)}) collective-permute-start(s32[3,256]{1,0:T(4,128)S(1)} %copy-done.7), channel_id=1, source_target_pairs={{0,12},{4,16},{8,20},{12,24},{16,28},{20,32},{24,36},{28,40},{32,4... | collective-permute-start | bytes 9224 | tf_op jit(solution)/shard_map/ppermute | solution.py:23
  133.7 9.5 %collective-permute-start.10 = (s32[3,256]{1,0:T(4,128)S(1)}, s32[3,256]{1,0:T(4,128)S(1)}, u32[]{:S(2)}, u32[]{:S(2)}) collective-permute-start(s32[3,256]{1,0:T(4,128)S(1)} %copy-done.7), channel_id=1, source_target_pairs={{0,8},{4,12},{8,16},{12,20},{16,24},{20,28},{24,32},{28,36},{32,40... | collective-permute-start | bytes 9224 | tf_op jit(solution)/shard_map/ppermute | solution.py:23
  143.1 8.6 %collective-permute-start.11 = (s32[3,256]{1,0:T(4,128)S(1)}, s32[3,256]{1,0:T(4,128)S(1)}, u32[]{:S(2)}, u32[]{:S(2)}) collective-permute-start(s32[3,256]{1,0:T(4,128)S(1)} %copy-done.7), channel_id=1, source_target_pairs={{0,4},{4,8},{8,12},{12,16},{16,20},{20,24},{24,28},{28,32},{32,36}... | collective-permute-start | bytes 9224 | tf_op jit(solution)/shard_map/ppermute | solution.py:23
  151.7 4.6 %collective-permute-start.12 = (s32[3,256]{1,0:T(4,128)S(1)}, s32[3,256]{1,0:T(4,128)S(1)}, u32[]{:S(2)}, u32[]{:S(2)}) collective-permute-start(s32[3,256]{1,0:T(4,128)S(1)} %copy-done.7), channel_id=1, source_target_pairs={{0,508},{4,0},{8,4},{12,8},{16,12},{20,16},{24,20},{28,24},{32,28}... | collective-permute-start | bytes 9224 | tf_op jit(solution)/shard_map/ppermute | solution.py:23
  156.3 5.2 %collective-permute-start.13 = (s32[3,256]{1,0:T(4,128)S(1)}, s32[3,256]{1,0:T(4,128)S(1)}, u32[]{:S(2)}, u32[]{:S(2)}) collective-permute-start(s32[3,256]{1,0:T(4,128)S(1)} %copy-done.7), channel_id=1, source_target_pairs={{0,504},{4,508},{8,0},{12,4},{16,8},{20,12},{24,16},{28,20},{32,24... | collective-permute-start | bytes 9224 | tf_op jit(solution)/shard_map/ppermute | solution.py:23
  161.6 6.3 %collective-permute-start.14 = (s32[3,256]{1,0:T(4,128)S(1)}, s32[3,256]{1,0:T(4,128)S(1)}, u32[]{:S(2)}, u32[]{:S(2)}) collective-permute-start(s32[3,256]{1,0:T(4,128)S(1)} %copy-done.7), channel_id=1, source_target_pairs={{0,500},{4,504},{8,508},{12,0},{16,4},{20,8},{24,12},{28,16},{32,2... | collective-permute-start | bytes 9224 | tf_op jit(solution)/shard_map/ppermute | solution.py:23
  167.9 10.4 %collective-permute-start.15 = (s32[3,256]{1,0:T(4,128)S(1)}, s32[3,256]{1,0:T(4,128)S(1)}, u32[]{:S(2)}, u32[]{:S(2)}) collective-permute-start(s32[3,256]{1,0:T(4,128)S(1)} %copy-done.7), channel_id=1, source_target_pairs={{0,496},{4,500},{8,504},{12,508},{16,0},{20,4},{24,8},{28,12},{32,... | collective-permute-start | bytes 9224 | tf_op jit(solution)/shard_map/ppermute | solution.py:23
  178.2 42.0 %collective-permute-start.4 = (bf16[256,512]{1,0:T(8,128)(2,1)S(1)}, bf16[256,512]{1,0:T(8,128)(2,1)}, u32[]{:S(2)}, u32[]{:S(2)}) collective-permute-start(bf16[256,512]{1,0:T(8,128)(2,1)S(1)} %copy-done.5), channel_id=1, source_target_pairs={{0,508},{4,0},{8,4},{12,8},{16,12},{20,16},{24,20},{28,24},{32,28}... | collective-permute-start | bytes 786440 | tf_op jit(solution)/shard_map/ppermute | solution.py:23
  193.4 28.5 %collective-permute-start.5 = (bf16[256,512]{1,0:T(8,128)(2,1)S(1)}, bf16[256,512]{1,0:T(8,128)(2,1)}, u32[]{:S(2)}, u32[]{:S(2)}) collective-permute-start(bf16[256,512]{1,0:T(8,128)(2,1)S(1)} %copy-done.5), channel_id=1, source_target_pairs={{0,504},{4,508},{8,0},{12,4},{16,8},{20,12},{24,16},{28,20},{32,24... | collective-permute-start | bytes 786440 | tf_op jit(solution)/shard_map/ppermute | solution.py:23
  197.0 43.7 %collective-permute-start.6 = (bf16[256,512]{1,0:T(8,128)(2,1)S(1)}, bf16[256,512]{1,0:T(8,128)(2,1)}, u32[]{:S(2)}, u32[]{:S(2)}) collective-permute-start(bf16[256,512]{1,0:T(8,128)(2,1)S(1)} %copy-done.5), channel_id=1, source_target_pairs={{0,500},{4,504},{8,508},{12,0},{16,4},{20,8},{24,12},{28,16},{32,2... | collective-permute-start | bytes 786440 | tf_op jit(solution)/shard_map/ppermute | solution.py:23
  200.5 41.8 %collective-permute-start.7 = (bf16[256,512]{1,0:T(8,128)(2,1)S(1)}, bf16[256,512]{1,0:T(8,128)(2,1)}, u32[]{:S(2)}, u32[]{:S(2)}) collective-permute-start(bf16[256,512]{1,0:T(8,128)(2,1)S(1)} %copy-done.5), channel_id=1, source_target_pairs={{0,496},{4,500},{8,504},{12,508},{16,0},{20,4},{24,8},{28,12},{32,... | collective-permute-start | bytes 786440 | tf_op jit(solution)/shard_map/ppermute | solution.py:23
  204.9 11.2 %all-to-all-start.1 = ((f32[8,16,256]{2,1,0:T(8,128)}), f32[8,16,256]{2,1,0:T(8,128)S(1)}, u32[]{:S(2)}, u32[]{:S(2)}) async-start(f32[8,16,256]{2,1,0:T(8,128)} %reduce_sum.52), calls=%async_computation.1 | async-start | bytes 262144 | tf_op jit(solution)/shard_map/all_to_all | solution.py:41
  216.8 11.2 %all-to-all-start.2 = ((f32[8,16,256]{2,1,0:T(8,128)}), f32[8,16,256]{2,1,0:T(8,128)S(1)}, u32[]{:S(2)}, u32[]{:S(2)}) async-start(f32[8,16,256]{2,1,0:T(8,128)} %broadcast_in_dim.30), calls=%async_computation.2 | async-start | bytes 262144 | tf_op jit(solution)/shard_map/all_to_all | solution.py:54
  229.7 14.4 %copy-start.1 = (bf16[2,512,512]{2,1,0:T(8,128)(2,1)S(1)}, bf16[2,512,512]{2,1,0:T(8,128)(2,1)}, u32[]{:S(2)}) copy-start(bf16[2,512,512]{2,1,0:T(8,128)(2,1)} %param.17) | copy-start | bytes 3145732
  229.7 14.4 %copy-start.11 = (f32[2]{0:T(128)S(1)}, f32[2]{0:T(128)}, u32[]{:S(2)}) copy-start(f32[2]{0:T(128)} %param.16) | copy-start | bytes 28
  229.7 49.5 %all-to-all-start.3 = ((f32[16,8,16,256]{3,2,1,0:T(8,128)}), f32[16,8,16,256]{3,2,1,0:T(8,128)}, u32[]{:S(2)}, u32[]{:S(2)}) async-start(f32[16,8,16,256]{3,2,1,0:T(8,128)} %broadcast_in_dim.31), calls=%async_computation.3 | async-start | bytes 4194304 | tf_op jit(solution)/shard_map/all_to_all | solution.py:54
  262.7 18.4 %copy-start.2 = (f32[1024,256]{1,0:T(8,128)S(1)}, f32[1024,256]{1,0:T(8,128)}, u32[]{:S(2)}) copy-start(f32[1024,256]{1,0:T(8,128)} %multiply_exponential_fusion) | copy-start | bytes 3145732
  279.2 1.9 copy-start.6
  281.0 1.8 copy-start.4
where the time goes:
time: 309 us; the launch traced here: 308 us
  waiting for transfers between devices  138 us (45%)
  starting transfers between devices  94.3 us (31%)
  local copies, waits for them, and re-layouts  27.8 us (9%)
  blocking collectives  22.4 us (7%)
  other arithmetic  11.2 us (4%)
  matrix products  9.32 us (3%)
  loops' own time  3.95 us (1%)
    ppermute x16, waiting for transfers between devices, shifted(): return lax.ppermute(value, axis, pairs)  111 us
    ppermute x16, starting transfers between devices, shifted(): return lax.ppermute(value, axis, pairs)  67.7 us
    all_to_all x1, blocking collectives, sent_and_summed(): lax.all_to_all(in_blocks(value, dim, count), axis, 0, 0, tiled=True)  22.4 us
    all_to_all x2, waiting for transfers between devices, copy_for_each(): return lax.all_to_all(copies, axis, split_axis=0, concat_axis=0, tiled=True)  21 us
    all_to_all x2, starting transfers between devices, copy_for_each(): return lax.all_to_all(copies, axis, split_axis=0, concat_axis=0, tiled=True)  14.4 us
    unnamed x40, local copies, waits for them, and re-layouts  11.6 us
    all_to_all x1, starting transfers between devices, sum_at_owner(): lax.all_to_all(pieces, axis, split_axis=0, concat_axis=0, tiled=True)  8.81 us
    all_to_all x1, waiting for transfers between devices, summed_rows(): lax.all_to_all(nearer, far, split_axis=0, concat_axis=0, tiled=True)  6.37 us
  transfers between devices with their start and end apart: 20, of which 11 were waited for; matrix products, arithmetic and copies ran while one was open for 10% of the time, Pallas kernels for 0%

commit v1 on v0

v1 whole, which is shorter than its diff:
```python
import math

import jax
import jax.numpy as jnp
from jax import lax
from jax.experimental import pallas as pl
from jax.experimental.pallas import tpu as pltpu
from jax.sharding import Mesh
from jax.sharding import PartitionSpec as P

K = 4096
RADIAL = 8
BLOCK = 128
NBR = 12
NATOMS = 32768
CUTOFF = 0.5
ATOMS = ("z", "xlo", "y")
WAVES = ("xhi", "core")
ROWS = 144

SIN_PI = (
    3.1415926535362884,
    -5.167712764624537,
    2.5501633189471584,
    -0.5992521978252471,
    0.08205040181554192,
    -0.00702838642033113,
)


def sin_pi(v):
    square = v * v
    total = jnp.float32(SIN_PI[-1])
    for coefficient in SIN_PI[-2::-1]:
        total = total * square + jnp.float32(coefficient)
    return total * v


def phases_of(waves, spots):
    turn = (
        waves[0][:, None] * spots[0][None, :]
        + waves[1][:, None] * spots[1][None, :]
        + waves[2][:, None] * spots[2][None, :]
    )
    share = turn * (1.0 / 65536.0)
    share = share - jnp.floor(share + 0.5)
    cosine = sin_pi(0.5 - 2.0 * jnp.abs(share))
    shifted = share - 0.25
    shifted = shifted - jnp.floor(shifted + 0.5)
    sine = sin_pi(0.5 - 2.0 * jnp.abs(shifted))
    return jnp.concatenate([cosine, sine], axis=0).astype(jnp.bfloat16)


def short_kernel(slots, coef, own, window, weight, out, spread, source):
    for block in range(2):
        rows = slice(block * BLOCK, (block + 1) * BLOCK)
        for j in range(NBR):
            slot = slots[block, j]
            near = window[slot, BLOCK : BLOCK + 16, :].astype(jnp.float32)
            dist_sq = None
            for axis in range(3):
                spot = near[axis : axis + 1] * 256.0 + near[axis + 3 : axis + 4]
                gap = own[rows, axis : axis + 1] - spot
                gap = gap - 65536.0 * jnp.floor(gap * (1.0 / 65536.0) + 0.5)
                gap = gap * (1.0 / 65536.0)
                dist_sq = gap * gap if dist_sq is None else dist_sq + gap * gap
            distance = jnp.sqrt(dist_sq)
            fade = 1.0 - dist_sq * 4.0
            smooth = jnp.where(
                dist_sq < CUTOFF * CUTOFF, fade * fade * (1.0 / math.sqrt(NBR * BLOCK)), 0.0
            )
            for r in range(RADIAL):
                shaped = (distance - CUTOFF * r / (RADIAL - 1)) * coef[0, r]
                value = jnp.exp(-(shaped * shaped)) * smooth
                spread[r * BLOCK : (r + 1) * BLOCK, j * BLOCK : (j + 1) * BLOCK] = value.astype(
                    jnp.bfloat16
                )
            source[j * BLOCK : (j + 1) * BLOCK, :] = window[slot, 0:BLOCK, :]
        gathered = jnp.dot(spread[...], source[...], preferred_element_type=jnp.float32)
        gathered = gathered.astype(jnp.bfloat16)
        gathered = jnp.concatenate(
            [gathered[r * BLOCK : (r + 1) * BLOCK] for r in range(RADIAL)], axis=1
        )
        out[rows, :] = jnp.dot(gathered, weight[...], preferred_element_type=jnp.float32)


def short_range_of(slots, coef, own, window, weight):
    return pl.pallas_call(
        short_kernel,
        out_shape=jax.ShapeDtypeStruct((2 * BLOCK, weight.shape[1]), jnp.float32),
        in_specs=[
            pl.BlockSpec(memory_space=pltpu.SMEM),
            pl.BlockSpec(memory_space=pltpu.SMEM),
            pl.BlockSpec(memory_space=pltpu.VMEM),
            pl.BlockSpec(memory_space=pltpu.VMEM),
            pl.BlockSpec(memory_space=pltpu.VMEM),
        ],
        out_specs=pl.BlockSpec(memory_space=pltpu.VMEM),
        scratch_shapes=[
            pltpu.VMEM((RADIAL * BLOCK, NBR * BLOCK), jnp.bfloat16),
            pltpu.VMEM((NBR * BLOCK, BLOCK), jnp.bfloat16),
        ],
        cost_estimate=pl.CostEstimate(
            flops=1100000000, bytes_accessed=3000000, transcendentals=3500000
        ),
        name="short_range",
    )(slots, coef, own, window, weight)


def exchanged(pieces, axes):
    return lax.all_to_all(pieces, axes, split_axis=0, concat_axis=0, tiled=True)


def coded(spots):
    digits = jnp.concatenate([spots >> 8, spots & 255], axis=0)
    return digits.astype(jnp.bfloat16)


def local(
    features,
    positions,
    neighbours,
    wavevectors,
    radial_width,
    short_weight,
    latent_weight,
    mix_weight,
    filter_rate,
    out_weight,
):
    xlo = lax.axis_index("xlo")
    y = lax.axis_index("y")
    wave = lax.axis_index(WAVES)
    atoms, channels = features.shape
    latents = latent_weight.shape[1]
    rows_count = lax.axis_size("z") * lax.axis_size("xlo")
    columns = lax.axis_size("y")
    wave_devices = lax.axis_size(WAVES)
    part = channels // wave_devices

    latent = jnp.dot(features, latent_weight, preferred_element_type=jnp.float32).astype(
        jnp.bfloat16
    )
    digits = coded(positions)
    packet = jnp.concatenate(
        [latent, digits, jnp.zeros((10, latents), jnp.bfloat16)], axis=0
    )
    arrived = lax.ppermute(packet, "xlo", [(0, 1), (1, 0)])
    other_latent = arrived[:atoms]
    other_digits = arrived[atoms : atoms + 6].astype(jnp.float32)
    other_spots = other_digits[0:3] * 256.0 + other_digits[3:6]

    own_part = lax.dynamic_slice_in_dim(features, wave * part, part, axis=1)
    block_digits = jnp.moveaxis(digits.reshape(6, 2, BLOCK), 1, 0)
    block_digits = jnp.pad(block_digits, ((0, 0), (0, ROWS - BLOCK - 6), (0, 0)))
    mine = jnp.concatenate([own_part.reshape(2, BLOCK, part), block_digits], axis=1)
    pairs = [
        (
            row * columns + column,
            (row + (-1 if column < columns // 2 else 1)) % rows_count * columns + column,
        )
        for row in range(rows_count)
        for column in range(columns)
    ]
    beside = lax.ppermute(mine, ATOMS, pairs)

    ahead = y - jnp.arange(columns, dtype=jnp.int32)
    use_mine = jnp.stack(
        [(ahead > -4) & (ahead <= 4), (ahead >= -4) & (ahead < 4)], axis=1
    )
    window = jnp.where(use_mine[:, :, None, None], mine[None], beside[None])
    window = exchanged(window, "y").reshape(2 * columns, ROWS, part)

    high = lax.reduce_precision(radial_width, 8, 7)
    middle = lax.reduce_precision(radial_width - high, 8, 7)
    low = radial_width - high - middle
    widths = jnp.stack([high, middle, low]).reshape(1, 6).astype(jnp.bfloat16)
    widths = jnp.pad(widths, ((0, 15), (0, channels - 6)))
    maps = jnp.moveaxis(short_weight.reshape(2, wave_devices, part, channels), 1, 0)
    maps = maps.reshape(wave_devices, 2 * part, channels)
    maps = jnp.concatenate(
        [maps, jnp.broadcast_to(widths, (wave_devices, 16, channels))], axis=1
    )
    maps = exchanged(maps, WAVES)
    width_digits = maps[:, 2 * part, :6].astype(jnp.float32).reshape(wave_devices, 3, 2)
    width = (width_digits[:, 0] + width_digits[:, 1] + width_digits[:, 2]).reshape(1, RADIAL)
    flat_weight = maps[:, : 2 * part].reshape(RADIAL * part, channels)

    spots = positions.astype(jnp.float32)
    own_columns = jnp.pad(spots.T, ((0, 0), (0, 5)))
    short_range = short_range_of(
        neighbours & (2 * columns - 1), 1.0 / width, own_columns, window, flat_weight
    )

    half = wavevectors.shape[1] // 2
    waves = lax.dynamic_slice_in_dim(wavevectors, xlo * half, half, axis=1)
    float_waves = waves.astype(jnp.float32)
    own_phases = phases_of(float_waves, spots)
    other_phases = phases_of(float_waves, other_spots)
    partial = jnp.dot(own_phases, latent, preferred_element_type=jnp.float32) + jnp.dot(
        other_phases, other_latent, preferred_element_type=jnp.float32
    )
    owners = ("z", "y")
    count = lax.axis_size(owners)
    lines = 2 * half // count
    pieces = exchanged(partial.astype(jnp.bfloat16).reshape(count, lines, latents), owners)
    factors = jnp.sum(pieces.astype(jnp.float32), axis=0)
    mixed = jnp.dot(factors, mix_weight, precision=lax.Precision.HIGHEST)
    first = lax.rem(lax.axis_index(owners) * lines, half)
    filter_waves = lax.dynamic_slice_in_dim(waves, first, lines, axis=1)
    lengths = jnp.sum(filter_waves * filter_waves, axis=0).astype(jnp.float32)
    gain = jnp.exp(-lengths[:, None] * filter_rate[None, :])
    filtered = (gain * mixed * (1.0 / math.sqrt(NATOMS))).astype(jnp.bfloat16)
    filtered = exchanged(jnp.broadcast_to(filtered, (count, lines, latents)), owners)
    filtered = filtered.reshape(2 * half, latents)

    def back(phases):
        summed = lax.dot_general(
            phases, filtered, (((0,), (0,)), ((), ())), preferred_element_type=jnp.float32
        )
        summed = (summed * (1.0 / math.sqrt(K))).astype(jnp.bfloat16)
        return jnp.dot(summed, out_weight, preferred_element_type=jnp.float32)

    own_message = (back(own_phases) + short_range).astype(jnp.bfloat16)
    other_message = back(other_phases).astype(jnp.bfloat16)
    first_is_mine = xlo == 0
    message = jnp.stack(
        [
            jnp.where(first_is_mine, own_message, other_message),
            jnp.where(first_is_mine, other_message, own_message),
        ]
    )
    message = jnp.moveaxis(message.reshape(2, atoms, wave_devices, part), 2, 1)
    message = exchanged(message.reshape(2 * wave_devices, atoms, part), ("xlo", *WAVES))
    return jnp.sum(message.astype(jnp.float32), axis=0).astype(jnp.bfloat16)


def solution(mesh):
    torus = Mesh(mesh.devices.reshape(8, 2, 8, 2, 2), (*ATOMS, *WAVES))
    placed = (
        P(ATOMS, None),
        P(None, ATOMS),
        P(ATOMS, None),
        P(None, WAVES),
        P(WAVES),
        P(WAVES, None, None),
        P(),
        P(),
        P(),
        P(),
    )
    return jax.shard_map(
        local, mesh=torus, in_specs=placed, out_specs=P(ATOMS, WAVES), check_vma=False
    )
```

time: 309 us -> 132 us (0.43)
  waiting for transfers between devices: 138 us -> 45.4 us
  starting transfers between devices: 94.3 us -> 41.7 us
  local copies, waits for them, and re-layouts: 27.8 us -> 6.31 us
  Pallas kernels: 0 us -> 9.02 us
  blocking collectives: 22.4 us -> 13.6 us
  loops' own time: 3.95 us -> 0 us
  other arithmetic: 11.2 us -> 7.8 us
    ppermute x16 -> x2, waiting for transfers between devices: 111 us -> 7.36 us  [the longest x1 7.35 us: local(): beside = lax.ppermute(mine, ATOMS, pairs)]
    ppermute x16 -> x2, starting transfers between devices: 67.7 us -> 8 us  [the longest x1 4.06 us: local(): beside = lax.ppermute(mine, ATOMS, pairs)]
    unnamed x40 -> x16, local copies, waits for them, and re-layouts: 11.6 us -> 0.17 us
    all_to_all x4, waiting for transfers between devices: 27.3 us -> 38.1 us  [exchanged(): return lax.all_to_all(pieces, axes, split_axis=0, concat_axis=0, tiled=True)]
    pallas_call x0 -> x1, Pallas kernels: none -> 9.02 us  [short_range_of(): pl.pallas_call(short_kernel, out_shape=jax.ShapeDtypeStruct((2 * BLOCK, w...]
    all_to_all x1, blocking collectives: 22.4 us -> 13.6 us  [exchanged(): return lax.all_to_all(pieces, axes, split_axis=0, concat_axis=0, tiled=True)]
    all_to_all x4, starting transfers between devices: 26.6 us -> 33.7 us  [exchanged(): return lax.all_to_all(pieces, axes, split_axis=0, concat_axis=0, tiled=True)]
    gather x6 -> x0, local copies, waits for them, and re-layouts: 5.79 us -> none  [the longest x2 4.63 us: short_block(): near_feat = window_feat[near_blocks]]
  transfers between devices with their start and end apart: 20 -> 6, of which waited for: 11 -> 5; matrix products, arithmetic and copies ran while one was open for 10% -> 11% of each run, Pallas kernels for 0% -> 7%
where the time goes in v1:
time: 132 us; the launch traced here: 131 us
  waiting for transfers between devices  45.4 us (34%)
  starting transfers between devices  41.7 us (32%)
  blocking collectives  13.6 us (10%)
  Pallas kernels  9.02 us (7%)
  other arithmetic  7.8 us (6%)
  matrix products  7.15 us (5%)
  local copies, waits for them, and re-layouts  6.31 us (5%)
    all_to_all x4, waiting for transfers between devices, exchanged(): return lax.all_to_all(pieces, axes, split_axis=0, concat_axis=0, tiled=True)  38.1 us
    all_to_all x4, starting transfers between devices, exchanged(): return lax.all_to_all(pieces, axes, split_axis=0, concat_axis=0, tiled=True)  33.7 us
    all_to_all x1, blocking collectives, exchanged(): return lax.all_to_all(pieces, axes, split_axis=0, concat_axis=0, tiled=True)  13.6 us
    pallas_call x1, Pallas kernels, short_range_of(): pl.pallas_call(short_kernel, out_shape=jax.ShapeDtypeStruct((2 * BLOCK, w...  9.02 us
    ppermute x1, waiting for transfers between devices, local(): beside = lax.ppermute(mine, ATOMS, pairs)  7.35 us
    ppermute x1, starting transfers between devices, local(): beside = lax.ppermute(mine, ATOMS, pairs)  4.06 us
    ppermute x1, starting transfers between devices, local(): arrived = lax.ppermute(packet, 'xlo', [(0, 1), (1, 0)])  3.94 us
    dot_general x2, matrix products, back(): return jnp.dot(summed, out_weight, preferred_element_type=jnp.float32)  3.26 us
  transfers between devices with their start and end apart: 6, of which 5 were waited for; matrix products, arithmetic and copies ran while one was open for 11% of the time, Pallas kernels for 7%

profile of v1, /device:TPU:1, one launch (start us, length us, event | category | flops | bytes accessed | tf_op | source)
XLA Modules:
  0.0 131.3 jit_solution(10789487096140189719)
XLA Ops:
  0.0 0.7 shift-right-arithmetic_convert_fusion
  0.7 1.2 convolution_convert_fusion.1
  2.2 3.9 %collective-permute-start = (bf16[272,256]{1,0:T(8,128)(2,1)S(1)}, bf16[272,256]{1,0:T(8,128)(2,1)S(1)}, u32[]{:S(2)}, u32[]{:S(2)}) collective-permute-start(bf16[272,256]{1,0:T(8,128)(2,1)S(1)} %maximum_maximum_fusion), channel_id=1, source_target_pairs={{0,32},{32,0},{1,33},{33,1},{2,34},{34,2},{3,35},{35,3},{4,36},{36... | collective-permute-start | bytes 417800 | tf_op jit(solution)/shard_map/ppermute | solution.py:148
  6.1 0.7 fusion.35
  6.9 1.3 copy.27
  8.2 1.1 pad_maximum_fusion
  9.3 8.4 %all-to-all-start.2 = ((bf16[4,272,512]{2,1,0:T(8,128)(2,1)}), bf16[4,272,512]{2,1,0:T(8,128)(2,1)S(1)}, u32[]{:S(2)}, u32[]{:S(2)}) async-start(bf16[4,272,512]{2,1,0:T(8,128)(2,1)} %pad_maximum_fusion), calls=%async_computation.2 | async-start | bytes 2228224 | tf_op jit(solution)/shard_map/all_to_all | solution.py:111
  17.9 0.7 convert_bitcast_fusion
  18.9 1.7 %multiply_convert_fusion.1 = (bf16[512,256]{1,0:T(8,128)(2,1)S(1)}, bf16[512,256]{1,0:T(8,128)(2,1)S(1)}, bf16[512,256]{1,0:T(8,128)(2,1)S(1)}, bf16[512,256]{1,0:T(8,128)(2,1)S(1)}) fusion(f32[256]{0:T(256)S(1)} %bitcast.53, f32[256]{0:T(256)S(1)} %bitcast.54, f32[256]{0:T(256)S(1)} %bitcast.52, f32[512]{0:T(512)S(1)} %bitcast.50, f32[512]{0:T(512)S(1)} %bitcast.51, ...), kind=kLoop, calls=%fused_computation.33 | loop fusion | flops 11796480 | bytes 1060864 | tf_op jit(solution)/shard_map/convert.12
  20.9 1.1 fusion
  22.1 11.4 %all-to-all-done.2 = bf16[4,272,512]{2,1,0:T(8,128)(2,1)S(1)} async-done(((bf16[4,272,512]{2,1,0:T(8,128)(2,1)}), bf16[4,272,512]{2,1,0:T(8,128)(2,1)S(1)}, u32[]{:S(2)}, u32[]{:S(2)}) %all-to-all-start.2) | async-done | bytes 1114144 | tf_op jit(solution)/shard_map/all_to_all | solution.py:111
  33.4 12.9 %all-to-all-start = ((bf16[64,16,256]{2,1,0:T(8,128)(2,1)}), bf16[64,16,256]{2,1,0:T(8,128)(2,1)S(1)}, u32[]{:S(2)}, u32[]{:S(2)}) async-start(bf16[64,16,256]{2,1,0:T(8,128)(2,1)} %bitcast.6), calls=%async_computation | async-start | bytes 1048576 | tf_op jit(solution)/shard_map/all_to_all | solution.py:111
  46.5 0.9 constant_dynamic-slice_fusion
  47.3 4.1 %collective-permute-start.1 = (bf16[2,144,128]{2,1,0:T(8,128)(2,1)S(1)}, bf16[2,144,128]{2,1,0:T(8,128)(2,1)S(1)}, u32[]{:S(2)}, u32[]{:S(2)}) collective-permute-start(bf16[2,144,128]{2,1,0:T(8,128)(2,1)S(1)} %fusion.27), channel_id=1, source_target_pairs={{0,480},{4,484},{8,488},{12,492},{16,48},{20,52},{24,56},{28,60},{... | collective-permute-start | bytes 221192 | tf_op jit(solution)/shard_map/ppermute | solution.py:165
  51.5 7.4 %collective-permute-done.1 = bf16[2,144,128]{2,1,0:T(8,128)(2,1)S(1)} collective-permute-done((bf16[2,144,128]{2,1,0:T(8,128)(2,1)S(1)}, bf16[2,144,128]{2,1,0:T(8,128)(2,1)S(1)}, u32[]{:S(2)}, u32[]{:S(2)}) %collective-permute-start.1) | collective-permute-done | bytes 73760 | tf_op jit(solution)/shard_map/ppermute | solution.py:165
  58.8 0.9 broadcast_select_fusion
  59.8 3.5 %all-to-all-done = bf16[64,16,256]{2,1,0:T(8,128)(2,1)S(1)} async-done(((bf16[64,16,256]{2,1,0:T(8,128)(2,1)}), bf16[64,16,256]{2,1,0:T(8,128)(2,1)S(1)}, u32[]{:S(2)}, u32[]{:S(2)}) %all-to-all-start) | async-done | bytes 524320 | tf_op jit(solution)/shard_map/all_to_all | solution.py:111
  63.2 6.6 %all-to-all-start.3 = ((bf16[8,2,144,128]{3,2,1,0:T(8,128)(2,1)}), bf16[8,2,144,128]{3,2,1,0:T(8,128)(2,1)S(1)}, u32[]{:S(2)}, u32[]{:S(2)}) async-start(bf16[8,2,144,128]{3,2,1,0:T(8,128)(2,1)} %broadcast_select_fusion), calls=%async_computation.3 | async-start | bytes 1179648 | tf_op jit(solution)/shard_map/all_to_all | solution.py:111
  70.1 1.2 fusion.5
  71.3 17.9 %all-to-all-done.3 = bf16[8,2,144,128]{3,2,1,0:T(8,128)(2,1)S(1)} async-done(((bf16[8,2,144,128]{3,2,1,0:T(8,128)(2,1)}), bf16[8,2,144,128]{3,2,1,0:T(8,128)(2,1)S(1)}, u32[]{:S(2)}, u32[]{:S(2)}) %all-to-all-start.3) | async-done | bytes 589856 | tf_op jit(solution)/shard_map/all_to_all | solution.py:111
  89.2 0.9 broadcast_in_dim.39
  90.1 5.7 %all-to-all-start.1 = ((bf16[64,16,256]{2,1,0:T(8,128)(2,1)}), bf16[64,16,256]{2,1,0:T(8,128)(2,1)}, u32[]{:S(2)}, u32[]{:S(2)}) async-start(bf16[64,16,256]{2,1,0:T(8,128)(2,1)} %broadcast_in_dim.39), calls=%async_computation.1 | async-start | bytes 1048576 | tf_op jit(solution)/shard_map/all_to_all | solution.py:111
  95.8 0.7 pad.13.own
  96.5 0.6 broadcast_and_fusion.slots
  97.3 0.7 div.6.coef
  97.9 1.1 slice.108
  99.0 9.0 %short_range.1 = f32[256,512]{1,0:T(8,128)} custom-call(s32[2,12]{1,0:T(2,128)} %broadcast_and_fusion.slots, f32[1,8]{1,0:T(1,128)} %div.6.coef, f32[256,8]{1,0:T(8,128)} %pad.13.own, bf16[16,144,128]{2,1,0:T(8,128)(2,1)} %bitcast.47, bf16[1024,512]{1,0:T(8,128)(2,1)} %bitcast.46), custom_call_target="tpu_custom_call" | custom-call | flops 1100000000 | bytes 3000000 | tf_op jit(solution)/shard_map/short_range/pallas_call | solution.py:88
  108.0 5.3 %all-to-all-done.1 = bf16[64,16,256]{2,1,0:T(8,128)(2,1)} async-done(((bf16[64,16,256]{2,1,0:T(8,128)(2,1)}), bf16[64,16,256]{2,1,0:T(8,128)(2,1)}, u32[]{:S(2)}, u32[]{:S(2)}) %all-to-all-start.1) | async-done | bytes 524320 | tf_op jit(solution)/shard_map/all_to_all | solution.py:111
  113.3 1.6 %convolution_convert_fusion = bf16[256,512]{1,0:T(8,128)(2,1)S(1)} fusion(bf16[256,512]{1,0:T(8,128)(2,1)S(1)} %copy-done, bf16[1024,256]{1,0:T(8,128)(2,1)} %bitcast.7, bf16[512,256]{1,0:T(8,128)(2,1)S(1)} %get-tuple-element.16, bf16[512,256]{1,0:T(8,128)(2,1)S(1)} %get-tuple-element.15), kind=kOutput, calls=%fused_computation.2 | convolution fusion | flops 202637312 | bytes 1572864 | tf_op jit(solution)/shard_map/dot_general | solution.py:222
  115.0 1.7 %fusion.3 = f32[256,512]{1,0:T(8,128)S(1)} fusion(bf16[256,512]{1,0:T(8,128)(2,1)S(1)} %copy-done, bf16[1024,256]{1,0:T(8,128)(2,1)} %bitcast.7, bf16[512,256]{1,0:T(8,128)(2,1)S(1)} %get-tuple-element.22, bf16[512,256]{1,0:T(8,128)(2,1)S(1)} %get-tuple-element.23), kind=kOutput, calls=%fused_computation.8 | convolution fusion | flops 202506240 | bytes 1835008 | tf_op jit(solution)/shard_map/dot_general | solution.py:222
  116.9 13.6 %all_to_all.25 = bf16[8,256,128]{2,1,0:T(8,128)(2,1)S(1)} all-to-all(bf16[8,256,128]{2,1,0:T(8,128)(2,1)S(1)} %bitcast.44), channel_id=1, replica_groups=mesh['z'=8,'xlo'=2,'y'=8,'xhi'=2,'core'=2] {'xlo','xhi','core'}, dimensions={0} | all-to-all | bytes 1048576 | tf_op jit(solution)/shard_map/all_to_all | solution.py:111
  130.6 0.7 reduce_sum.32
  (50 shorter events, 1.9 us)
Async XLA Ops:
  0.0 113.3 %copy-start = (bf16[256,512]{1,0:T(8,128)(2,1)S(1)}, bf16[256,512]{1,0:T(8,128)(2,1)}, u32[]{:S(2)}) copy-start(bf16[256,512]{1,0:T(8,128)(2,1)} %param.19) | copy-start | bytes 786436
  2.2 16.7 %collective-permute-start = (bf16[272,256]{1,0:T(8,128)(2,1)S(1)}, bf16[272,256]{1,0:T(8,128)(2,1)S(1)}, u32[]{:S(2)}, u32[]{:S(2)}) collective-permute-start(bf16[272,256]{1,0:T(8,128)(2,1)S(1)} %maximum_maximum_fusion), channel_id=1, source_target_pairs={{0,32},{32,0},{1,33},{33,1},{2,34},{34,2},{3,35},{35,3},{4,36},{36... | collective-permute-start | bytes 417800 | tf_op jit(solution)/shard_map/ppermute | solution.py:148
  9.3 8.4 %copy-start.4 = (s32[3,256]{1,0:T(4,128)S(1)}, s32[3,256]{1,0:T(4,128)}, u32[]{:S(2)}) copy-start(s32[3,256]{1,0:T(4,128)} %param.11) | copy-start | bytes 9220
  9.3 9.3 %copy-start.5 = (s32[3,1024]{1,0:T(4,128)S(1)}, s32[3,1024]{1,0:T(4,128)}, u32[]{:S(2)}) copy-start(s32[3,1024]{1,0:T(4,128)} %param.13) | copy-start | bytes 36868
  9.3 24.1 %all-to-all-start.2 = ((bf16[4,272,512]{2,1,0:T(8,128)(2,1)}), bf16[4,272,512]{2,1,0:T(8,128)(2,1)S(1)}, u32[]{:S(2)}, u32[]{:S(2)}) async-start(bf16[4,272,512]{2,1,0:T(8,128)(2,1)} %pad_maximum_fusion), calls=%async_computation.2 | async-start | bytes 2228224 | tf_op jit(solution)/shard_map/all_to_all | solution.py:111
  33.4 29.8 %all-to-all-start = ((bf16[64,16,256]{2,1,0:T(8,128)(2,1)}), bf16[64,16,256]{2,1,0:T(8,128)(2,1)S(1)}, u32[]{:S(2)}, u32[]{:S(2)}) async-start(bf16[64,16,256]{2,1,0:T(8,128)(2,1)} %bitcast.6), calls=%async_computation | async-start | bytes 1048576 | tf_op jit(solution)/shard_map/all_to_all | solution.py:111
  47.3 11.5 %collective-permute-start.1 = (bf16[2,144,128]{2,1,0:T(8,128)(2,1)S(1)}, bf16[2,144,128]{2,1,0:T(8,128)(2,1)S(1)}, u32[]{:S(2)}, u32[]{:S(2)}) collective-permute-start(bf16[2,144,128]{2,1,0:T(8,128)(2,1)S(1)} %fusion.27), channel_id=1, source_target_pairs={{0,480},{4,484},{8,488},{12,492},{16,48},{20,52},{24,56},{28,60},{... | collective-permute-start | bytes 221192 | tf_op jit(solution)/shard_map/ppermute | solution.py:165
  63.2 26.0 %all-to-all-start.3 = ((bf16[8,2,144,128]{3,2,1,0:T(8,128)(2,1)}), bf16[8,2,144,128]{3,2,1,0:T(8,128)(2,1)S(1)}, u32[]{:S(2)}, u32[]{:S(2)}) async-start(bf16[8,2,144,128]{3,2,1,0:T(8,128)(2,1)} %broadcast_select_fusion), calls=%async_computation.3 | async-start | bytes 1179648 | tf_op jit(solution)/shard_map/all_to_all | solution.py:111
  70.1 25.8 %copy-start.2 = (f32[256,3]{1,0:T(8,128)S(1)}, f32[256,3]{1,0:T(8,128)}, u32[]{:S(2)}) copy-start(f32[256,3]{1,0:T(8,128)} %get-tuple-element.13) | copy-start | bytes 9220
  70.1 26.4 %copy-start.6 = (s32[2,12]{1,0:T(2,128)S(1)}, s32[2,12]{1,0:T(2,128)}, u32[]{:S(2)}) copy-start(s32[2,12]{1,0:T(2,128)} %param.12) | copy-start | bytes 292
  89.2 9.8 %copy-start.1 = (bf16[8,2,144,128]{3,2,1,0:T(8,128)(2,1)}, bf16[8,2,144,128]{3,2,1,0:T(8,128)(2,1)S(1)}, u32[]{:S(2)}) copy-start(bf16[8,2,144,128]{3,2,1,0:T(8,128)(2,1)S(1)} %all-to-all-done.3) | copy-start | bytes 1769476
  90.1 23.2 %all-to-all-start.1 = ((bf16[64,16,256]{2,1,0:T(8,128)(2,1)}), bf16[64,16,256]{2,1,0:T(8,128)(2,1)}, u32[]{:S(2)}, u32[]{:S(2)}) async-start(bf16[64,16,256]{2,1,0:T(8,128)(2,1)} %broadcast_in_dim.39), calls=%async_computation.1 | async-start | bytes 1048576 | tf_op jit(solution)/shard_map/all_to_all | solution.py:111
  114.9 1.7 %copy-start.3 = (f32[256,512]{1,0:T(8,128)S(1)}, f32[256,512]{1,0:T(8,128)}, u32[]{:S(2)}) copy-start(f32[256,512]{1,0:T(8,128)} %short_range.1) | copy-start | bytes 1572868

commit v2 on v1

v2 whole, which is shorter than its diff:
```python
import math

import jax
import jax.numpy as jnp
from jax import lax
from jax.experimental import pallas as pl
from jax.experimental.pallas import tpu as pltpu
from jax.sharding import Mesh
from jax.sharding import PartitionSpec as P


K = 4096
RADIAL = 8
BLOCK = 128
NBR = 12
NATOMS = 32768
CUTOFF = 0.5
ATOMS = ("z", "xlo", "y")
WAVES = ("xhi", "core")
ROWS = 144

SIN_PI = (
    3.1415926535362884,
    -5.167712764624537,
    2.5501633189471584,
    -0.5992521978252471,
    0.08205040181554192,
    -0.00702838642033113,
)


def sin_pi(v):
    square = v * v
    total = jnp.float32(SIN_PI[-1])
    for coefficient in SIN_PI[-2::-1]:
        total = total * square + jnp.float32(coefficient)
    return total * v


def phases_of(waves, spots):
    turn = (
        waves[0][:, None] * spots[0][None, :]
        + waves[1][:, None] * spots[1][None, :]
        + waves[2][:, None] * spots[2][None, :]
    )
    share = turn * (1.0 / 65536.0)
    share = share - jnp.floor(share + 0.5)
    cosine = sin_pi(0.5 - 2.0 * jnp.abs(share))
    shifted = share - 0.25
    shifted = shifted - jnp.floor(shifted + 0.5)
    sine = sin_pi(0.5 - 2.0 * jnp.abs(shifted))
    return jnp.concatenate([cosine, sine], axis=0).astype(jnp.bfloat16)


WINDOW_ROWS = 2 * ROWS
MAP_ROWS = 8 * BLOCK + 16


def map_rows(ref, first):
    quarters = [ref[first + q * 256 : first + (q + 1) * 256, :] for q in range(4)]
    return jnp.concatenate(quarters, axis=1)


def prepare_kernel(
    table, width, features, positions, weights, latent_weight, packet, mine, left, right, maps0, maps2
):
    wave = table[0]
    latent = jnp.dot(features[...], latent_weight[...], preferred_element_type=jnp.float32)
    spots = positions[...]
    digits = jnp.concatenate(
        [spots >> 8, spots & 255, jnp.zeros((10, spots.shape[1]), jnp.int32)], axis=0
    )
    digits = digits.astype(jnp.float32).astype(jnp.bfloat16)
    atoms = latent.shape[0]
    packet[0:atoms, :] = latent.astype(jnp.bfloat16)
    packet[atoms : atoms + 16, :] = digits

    row = lax.broadcasted_iota(jnp.int32, (16, BLOCK), 0)
    sharp = jnp.where(row % 2 == 0, width[0], width[1])
    sharp = 1.0 / sharp
    high = sharp.astype(jnp.bfloat16).astype(jnp.float32)
    middle = (sharp - high).astype(jnp.bfloat16).astype(jnp.float32)
    low = sharp - high - middle
    sharp = jnp.where(row < 2, high, jnp.where(row < 4, middle, jnp.where(row < 6, low, 0.0)))
    sharp = sharp.astype(jnp.bfloat16)

    def put_maps(out, first, target):
        start = pl.multiple_of(target * BLOCK, BLOCK)
        for i in range(2):
            for q in range(4):
                at = first + q * 256 + i * BLOCK
                out[at : at + BLOCK, :] = weights[
                    i, pl.ds(start, BLOCK), q * BLOCK : (q + 1) * BLOCK
                ]
        out[first + 1024 : first + 1040, :] = sharp

    def put_window(out, target):
        start = pl.multiple_of(target * BLOCK, BLOCK)
        for block in range(2):
            rows = slice(block * BLOCK, (block + 1) * BLOCK)
            out[block * ROWS : block * ROWS + BLOCK, :] = features[rows, pl.ds(start, BLOCK)]
            out[block * ROWS + BLOCK : (block + 1) * ROWS, :] = digits[:, rows]

    put_window(mine, wave)
    put_window(left, wave ^ 1)
    put_maps(left, WINDOW_ROWS, wave ^ 1)
    put_window(right, wave ^ 3)
    put_maps(right, WINDOW_ROWS, wave ^ 3)
    put_maps(maps0, 0, wave)
    put_maps(maps2, 0, wave ^ 2)


def prepared(wave, radial_width, features, positions, short_weight, latent_weight):
    in_vmem = pl.BlockSpec(memory_space=pltpu.VMEM)
    in_smem = pl.BlockSpec(memory_space=pltpu.SMEM)
    atoms = features.shape[0]
    shapes = [
        (atoms + 16, latent_weight.shape[1]),
        (WINDOW_ROWS, BLOCK),
        (WINDOW_ROWS + MAP_ROWS, BLOCK),
        (WINDOW_ROWS + MAP_ROWS, BLOCK),
        (MAP_ROWS, BLOCK),
        (MAP_ROWS, BLOCK),
    ]
    return pl.pallas_call(
        prepare_kernel,
        out_shape=[jax.ShapeDtypeStruct(shape, jnp.bfloat16) for shape in shapes],
        in_specs=[in_smem, in_smem, in_vmem, in_vmem, in_vmem, in_vmem],
        out_specs=[in_vmem] * 6,
        cost_estimate=pl.CostEstimate(flops=67000000, bytes_accessed=3500000, transcendentals=0),
        name="prepare",
    )(wave, radial_width, features, positions, short_weight, latent_weight)


def short_kernel(table, before, left, mine, right, after, maps0, maps2, out, window, spread, source):
    window[0 : 5 * ROWS] = before[...]
    window[5 * ROWS : 7 * ROWS] = left[0:WINDOW_ROWS]
    window[7 * ROWS : 9 * ROWS] = mine[...]
    window[9 * ROWS : 11 * ROWS] = right[0:WINDOW_ROWS]
    window[11 * ROWS : 16 * ROWS] = after[...]
    maps = ((maps0, 0), (left, WINDOW_ROWS), (maps2, 0), (right, WINDOW_ROWS))
    wave = table[0, NBR]
    centers = []
    sharpness = []
    for p in range(4):
        ref, first = maps[p]
        digits = ref[first + 1024 : first + 1040, :].astype(jnp.float32)
        for i in range(2):
            kernel_id = (2 * (wave ^ p) + i).astype(jnp.float32)
            centers.append(kernel_id * (CUTOFF / (RADIAL - 1)))
            sharpness.append(digits[i : i + 1] + digits[i + 2 : i + 3] + digits[i + 4 : i + 5])
    for block in range(2):
        rows = slice(block * BLOCK, (block + 1) * BLOCK)
        digits = mine[block * ROWS + BLOCK : (block + 1) * ROWS, :].astype(jnp.float32)
        spots = digits[0:3] * 256.0 + digits[3:6]
        spots = jnp.concatenate([spots, jnp.zeros((BLOCK - 3, BLOCK), jnp.float32)], axis=0).T
        for j in range(NBR):
            start = pl.multiple_of(table[block, j] * ROWS, 16)
            near = window[pl.ds(start + BLOCK, 16), :].astype(jnp.float32)
            dist_sq = None
            for axis in range(3):
                spot = near[axis : axis + 1] * 256.0 + near[axis + 3 : axis + 4]
                gap = spots[:, axis : axis + 1] - spot
                gap = gap - 65536.0 * jnp.floor(gap * (1.0 / 65536.0) + 0.5)
                gap = gap * (1.0 / 65536.0)
                dist_sq = gap * gap if dist_sq is None else dist_sq + gap * gap
            distance = jnp.sqrt(dist_sq)
            fade = 1.0 - dist_sq * 4.0
            smooth = jnp.where(
                dist_sq < CUTOFF * CUTOFF, fade * fade * (1.0 / math.sqrt(NBR * BLOCK)), 0.0
            )
            for r in range(RADIAL):
                shaped = (distance - centers[r]) * sharpness[r]
                value = jnp.exp(-(shaped * shaped)) * smooth
                spread[r * BLOCK : (r + 1) * BLOCK, j * BLOCK : (j + 1) * BLOCK] = value.astype(
                    jnp.bfloat16
                )
            source[j * BLOCK : (j + 1) * BLOCK, :] = window[pl.ds(start, BLOCK), :]
        gathered = jnp.dot(spread[...], source[...], preferred_element_type=jnp.float32)
        gathered = gathered.astype(jnp.bfloat16)
        total = None
        for p in range(4):
            pair = jnp.concatenate(
                [
                    gathered[2 * p * BLOCK : (2 * p + 1) * BLOCK],
                    gathered[(2 * p + 1) * BLOCK : (2 * p + 2) * BLOCK],
                ],
                axis=1,
            )
            share = jnp.dot(pair, map_rows(*maps[p]), preferred_element_type=jnp.float32)
            total = share if total is None else total + share
        out[rows, :] = total


def short_range_of(table, before, left, mine, right, after, maps0, maps2):
    in_vmem = pl.BlockSpec(memory_space=pltpu.VMEM)
    return pl.pallas_call(
        short_kernel,
        out_shape=jax.ShapeDtypeStruct((2 * BLOCK, 4 * BLOCK), jnp.float32),
        in_specs=[pl.BlockSpec(memory_space=pltpu.SMEM)] + [in_vmem] * 7,
        out_specs=in_vmem,
        scratch_shapes=[
            pltpu.VMEM((16 * ROWS, BLOCK), jnp.bfloat16),
            pltpu.VMEM((RADIAL * BLOCK, NBR * BLOCK), jnp.bfloat16),
            pltpu.VMEM((NBR * BLOCK, BLOCK), jnp.bfloat16),
        ],
        cost_estimate=pl.CostEstimate(
            flops=1100000000, bytes_accessed=3000000, transcendentals=3500000
        ),
        name="short_range",
    )(table, before, left, mine, right, after, maps0, maps2)


def exchanged(pieces, axes):
    return lax.all_to_all(pieces, axes, split_axis=0, concat_axis=0, tiled=True)


def moved(value, steps, wave_flip=0, atom_flip=0):
    count = lax.axis_size(ATOMS)
    waves = lax.axis_size(WAVES)
    pairs = [
        (
            device * waves + wave,
            (((device ^ atom_flip) + steps) % count) * waves + (wave ^ wave_flip),
        )
        for device in range(count)
        for wave in range(waves)
    ]
    return lax.ppermute(value, ATOMS + WAVES, pairs)


def local(
    features,
    positions,
    neighbours,
    wavevectors,
    radial_width,
    short_weight,
    latent_weight,
    mix_weight,
    filter_rate,
    out_weight,
):
    xlo = lax.axis_index("xlo")
    device = lax.axis_index(ATOMS)
    wave = lax.axis_index(WAVES).astype(jnp.int32)
    atoms, channels = features.shape
    latents = latent_weight.shape[1]
    wave_devices = lax.axis_size(WAVES)
    part = channels // wave_devices
    partner = lax.axis_size("y")

    packet, mine, to_right, to_left, maps0, maps2 = prepared(
        wave.reshape(1), radial_width, features, positions, short_weight, latent_weight
    )
    latent = packet[:atoms]
    arrived = moved(packet, 0, 0, partner)
    other_latent = arrived[:atoms]
    other_digits = arrived[atoms : atoms + 6].astype(jnp.float32)
    other_spots = other_digits[0:3] * 256.0 + other_digits[3:6]

    left = moved(to_right, 1, 1)
    right = moved(to_left, -1, 3)
    maps2 = moved(maps2, 0, 2, partner)
    sent_on = jnp.concatenate([left[ROWS:WINDOW_ROWS], mine, right[:WINDOW_ROWS]])
    sent_back = jnp.concatenate([left[:WINDOW_ROWS], mine, right[:ROWS]])
    before = moved(sent_on, 3)
    after = moved(sent_back, -3)

    slots = (neighbours - (2 * device - 7)) & 15
    table = jnp.concatenate([slots, jnp.broadcast_to(wave, (2, 1))], axis=1)
    short_range = short_range_of(table, before, left, mine, right, after, maps0, maps2)

    spots = positions.astype(jnp.float32)
    half = wavevectors.shape[1] // 2
    waves = lax.dynamic_slice_in_dim(wavevectors, xlo * half, half, axis=1)
    float_waves = waves.astype(jnp.float32)
    own_phases = phases_of(float_waves, spots)
    other_phases = phases_of(float_waves, other_spots)
    partial = jnp.dot(own_phases, latent, preferred_element_type=jnp.float32) + jnp.dot(
        other_phases, other_latent, preferred_element_type=jnp.float32
    )
    owners = ("z", "y")
    count = lax.axis_size(owners)
    lines = 2 * half // count
    pieces = exchanged(partial.astype(jnp.bfloat16).reshape(count, lines, latents), owners)
    factors = jnp.sum(pieces.astype(jnp.float32), axis=0)
    mixed = jnp.dot(factors, mix_weight, precision=lax.Precision.HIGHEST)
    first = lax.rem(lax.axis_index(owners) * lines, half)
    filter_waves = lax.dynamic_slice_in_dim(waves, first, lines, axis=1)
    lengths = jnp.sum(filter_waves * filter_waves, axis=0).astype(jnp.float32)
    gain = jnp.exp(-lengths[:, None] * filter_rate[None, :])
    filtered = (gain * mixed * (1.0 / math.sqrt(NATOMS))).astype(jnp.bfloat16)
    filtered = exchanged(jnp.broadcast_to(filtered, (count, lines, latents)), owners)
    filtered = filtered.reshape(2 * half, latents)

    def back(phases):
        summed = lax.dot_general(
            phases, filtered, (((0,), (0,)), ((), ())), preferred_element_type=jnp.float32
        )
        summed = (summed * (1.0 / math.sqrt(K))).astype(jnp.bfloat16)
        return jnp.dot(summed, out_weight, preferred_element_type=jnp.float32)

    own_message = (back(own_phases) + short_range).astype(jnp.bfloat16)
    other_message = back(other_phases).astype(jnp.bfloat16)
    first_is_mine = xlo == 0
    message = jnp.stack(
        [
            jnp.where(first_is_mine, own_message, other_message),
            jnp.where(first_is_mine, other_message, own_message),
        ]
    )
    message = jnp.moveaxis(message.reshape(2, atoms, wave_devices, part), 2, 1)
    message = exchanged(message.reshape(2 * wave_devices, atoms, part), ("xlo", *WAVES))
    return jnp.sum(message.astype(jnp.float32), axis=0).astype(jnp.bfloat16)


def solution(mesh):
    torus = Mesh(mesh.devices.reshape(8, 2, 8, 2, 2), (*ATOMS, *WAVES))
    placed = (
        P(ATOMS, None),
        P(None, ATOMS),
        P(ATOMS, None),
        P(None, WAVES),
        P(WAVES),
        P(WAVES, None, None),
        P(),
        P(),
        P(),
        P(),
    )

    return jax.shard_map(
        local, mesh=torus, in_specs=placed, out_specs=P(ATOMS, WAVES), check_vma=False
    )
```

time: 132 us -> 133 us (level)
  the two profiles are of different devices: /device:TPU:1 before, /device:TPU:16 now
where the time goes in v2:
time: 133 us; the launch traced here: 132 us
  waiting for transfers between devices  51.2 us (38%)
  starting transfers between devices  46.1 us (35%)
  blocking collectives  13.5 us (10%)
  Pallas kernels  11.7 us (9%)
  local copies, waits for them, and re-layouts  3.58 us (3%)
  other arithmetic  2.97 us (2%)
  matrix products  2.75 us (2%)
    ppermute x6, waiting for transfers between devices, moved(): return lax.ppermute(value, ATOMS + WAVES, pairs)  33.3 us
    ppermute x6, starting transfers between devices, moved(): return lax.ppermute(value, ATOMS + WAVES, pairs)  23.8 us
    all_to_all x2, starting transfers between devices, exchanged(): return lax.all_to_all(pieces, axes, split_axis=0, concat_axis=0, tiled=True)  22.4 us
    all_to_all x2, waiting for transfers between devices, exchanged(): return lax.all_to_all(pieces, axes, split_axis=0, concat_axis=0, tiled=True)  18 us
    all_to_all x1, blocking collectives, exchanged(): return lax.all_to_all(pieces, axes, split_axis=0, concat_axis=0, tiled=True)  13.5 us
    pallas_call x1, Pallas kernels, short_range_of(): pl.pallas_call(short_kernel, out_shape=jax.ShapeDtypeStruct((2 * BLOCK, 4...  8.92 us
    pallas_call x1, Pallas kernels, prepared(): pl.pallas_call(prepare_kernel, out_shape=[jax.ShapeDtypeStruct(shape, jnp...  2.74 us
  transfers between devices with their start and end apart: 8, of which 6 were waited for; matrix products, arithmetic and copies ran while one was open for 1% of the time, Pallas kernels for 7%

profile of v2, /device:TPU:16, one launch (start us, length us, event | category | flops | bytes accessed | tf_op | source)
XLA Modules:
  0.0 132.2 jit_solution(620797800326883699)
XLA Ops:
  0.0 2.7 %prepare.1 = (bf16[272,256]{1,0:T(8,128)(2,1)}, bf16[288,128]{1,0:T(8,128)(2,1)}, bf16[1328,128]{1,0:T(8,128)(2,1)}, bf16[1328,128]{1,0:T(8,128)(2,1)}, bf16[104...) custom-call(s32[1]{0:T(128)} %bitcast.6.table, f32[2]{0:T(128)} %width.1, bf16[256,512]{1,0:T(8,128)(2,1)} %features.1, ...), custom_call_target="tpu_custom_call" | custom-call | flops 67000000 | bytes 3500000 | tf_op jit(solution)/shard_map/prepare/pallas_call | solution.py:125
  2.7 3.5 %collective-permute-start = (bf16[272,256]{1,0:T(8,128)(2,1)}, bf16[272,256]{1,0:T(8,128)(2,1)S(1)}, u32[]{:S(2)}, u32[]{:S(2)}) collective-permute-start(bf16[272,256]{1,0:T(8,128)(2,1)} %get-tuple-element.11), channel_id=1, source_target_pairs={{0,32},{1,33},{2,34},{3,35},{4,36},{5,37},{6,38},{7,39},{8,40},{9,... | collective-permute-start | bytes 417800 | tf_op jit(solution)/shard_map/ppermute | solution.py:229
  6.4 4.0 %collective-permute-done = bf16[272,256]{1,0:T(8,128)(2,1)S(1)} collective-permute-done((bf16[272,256]{1,0:T(8,128)(2,1)}, bf16[272,256]{1,0:T(8,128)(2,1)S(1)}, u32[]{:S(2)}, u32[]{:S(2)}) %collective-permute-start) | collective-permute-done | bytes 139296 | tf_op jit(solution)/shard_map/ppermute | solution.py:229
  10.4 1.7 %multiply_convert_fusion.1 = (bf16[512,256]{1,0:T(8,128)(2,1)S(1)}, bf16[512,256]{1,0:T(8,128)(2,1)S(1)}, bf16[512,256]{1,0:T(8,128)(2,1)S(1)}, bf16[512,256]{1,0:T(8,128)(2,1)S(1)}) fusion(f32[256]{0:T(256)S(1)} %bitcast.33, f32[256]{0:T(256)S(1)} %bitcast.34, f32[256]{0:T(256)S(1)} %bitcast.32, f32[512]{0:T(512)S(1)} %bitcast.27, f32[512]{0:T(512)S(1)} %bitcast.28, ...), kind=kLoop, calls=%fused_computation.30 | loop fusion | flops 11796480 | bytes 1060864 | tf_op jit(solution)/shard_map/convert.1
  12.2 0.3 fusion.19
  12.5 1.1 fusion
  13.6 16.5 %all-to-all-start = ((bf16[64,16,256]{2,1,0:T(8,128)(2,1)}), bf16[64,16,256]{2,1,0:T(8,128)(2,1)S(1)}, u32[]{:S(2)}, u32[]{:S(2)}) async-start(bf16[64,16,256]{2,1,0:T(8,128)(2,1)} %bitcast.10), calls=%async_computation | async-start | bytes 1048576 | tf_op jit(solution)/shard_map/all_to_all | solution.py:215
  30.1 0.1 multiply_reduce_fusion
  30.2 17.9 %all-to-all-done = bf16[64,16,256]{2,1,0:T(8,128)(2,1)S(1)} async-done(((bf16[64,16,256]{2,1,0:T(8,128)(2,1)}), bf16[64,16,256]{2,1,0:T(8,128)(2,1)S(1)}, u32[]{:S(2)}, u32[]{:S(2)}) %all-to-all-start) | async-done | bytes 524320 | tf_op jit(solution)/shard_map/all_to_all | solution.py:215
  48.1 0.1 convert_reduce_fusion
  48.2 0.2 fusion.5
  48.5 0.8 broadcast_in_dim.2
  49.3 5.9 %all-to-all-start.1 = ((bf16[64,16,256]{2,1,0:T(8,128)(2,1)}), bf16[64,16,256]{2,1,0:T(8,128)(2,1)S(1)}, u32[]{:S(2)}, u32[]{:S(2)}) async-start(bf16[64,16,256]{2,1,0:T(8,128)(2,1)} %broadcast_in_dim.2), calls=%async_computation.1 | async-start | bytes 1048576 | tf_op jit(solution)/shard_map/all_to_all | solution.py:215
  55.2 1.9 %collective-permute-start.1 = (bf16[1328,128]{1,0:T(8,128)(2,1)S(1)}, bf16[1328,128]{1,0:T(8,128)(2,1)S(1)}, u32[]{:S(2)}, u32[]{:S(2)}) collective-permute-start(bf16[1328,128]{1,0:T(8,128)(2,1)S(1)} %copy-done.12), channel_id=1, source_target_pairs={{0,5},{1,4},{2,7},{3,6},{4,9},{5,8},{6,11},{7,10},{8,13},{9,12},{1... | collective-permute-start | bytes 1019912 | tf_op jit(solution)/shard_map/ppermute | solution.py:229
  57.2 6.1 %collective-permute-start.2 = (bf16[1328,128]{1,0:T(8,128)(2,1)S(1)}, bf16[1328,128]{1,0:T(8,128)(2,1)S(1)}, u32[]{:S(2)}, u32[]{:S(2)}) collective-permute-start(bf16[1328,128]{1,0:T(8,128)(2,1)S(1)} %copy-done.11), channel_id=1, source_target_pairs={{0,511},{1,510},{2,509},{3,508},{4,3},{5,2},{6,1},{7,0},{8,7},{9,6... | collective-permute-start | bytes 1019912 | tf_op jit(solution)/shard_map/ppermute | solution.py:229
  63.3 3.1 %collective-permute-start.5 = (bf16[1040,128]{1,0:T(8,128)(2,1)S(1)}, bf16[1040,128]{1,0:T(8,128)(2,1)}, u32[]{:S(2)}, u32[]{:S(2)}) collective-permute-start(bf16[1040,128]{1,0:T(8,128)(2,1)S(1)} %copy-done.13), channel_id=1, source_target_pairs={{0,34},{1,35},{2,32},{3,33},{4,38},{5,39},{6,36},{7,37},{8,42},{9,... | collective-permute-start | bytes 798728 | tf_op jit(solution)/shard_map/ppermute | solution.py:229
  66.4 5.9 %collective-permute-done.1.left = bf16[1328,128]{1,0:T(8,128)(2,1)S(1)} collective-permute-done((bf16[1328,128]{1,0:T(8,128)(2,1)S(1)}, bf16[1328,128]{1,0:T(8,128)(2,1)S(1)}, u32[]{:S(2)}, u32[]{:S(2)}) %collective-permute-start.1) | collective-permute-done | bytes 340000 | tf_op jit(solution)/shard_map/ppermute | solution.py:229
  72.3 3.9 %collective-permute-done.2.right = bf16[1328,128]{1,0:T(8,128)(2,1)S(1)} collective-permute-done((bf16[1328,128]{1,0:T(8,128)(2,1)S(1)}, bf16[1328,128]{1,0:T(8,128)(2,1)S(1)}, u32[]{:S(2)}, u32[]{:S(2)}) %collective-permute-start.2) | collective-permute-done | bytes 340000 | tf_op jit(solution)/shard_map/ppermute | solution.py:229
  76.2 0.9 copy-done.4
  77.2 7.1 %collective-permute-start.4 = (bf16[720,128]{1,0:T(8,128)(2,1)S(1)}, bf16[720,128]{1,0:T(8,128)(2,1)S(1)}, u32[]{:S(2)}, u32[]{:S(2)}) collective-permute-start(bf16[720,128]{1,0:T(8,128)(2,1)S(1)} %get-tuple-element.22), channel_id=1, source_target_pairs={{0,500},{1,501},{2,502},{3,503},{4,504},{5,505},{6,506},{7,507},{8... | collective-permute-start | bytes 552968 | tf_op jit(solution)/shard_map/ppermute | solution.py:229
  84.3 2.1 %collective-permute-start.3 = (bf16[720,128]{1,0:T(8,128)(2,1)S(1)}, bf16[720,128]{1,0:T(8,128)(2,1)S(1)}, u32[]{:S(2)}, u32[]{:S(2)}) collective-permute-start(bf16[720,128]{1,0:T(8,128)(2,1)S(1)} %get-tuple-element.23), channel_id=1, source_target_pairs={{0,12},{1,13},{2,14},{3,15},{4,16},{5,17},{6,18},{7,19},{8,20},{9,... | collective-permute-start | bytes 552968 | tf_op jit(solution)/shard_map/ppermute | solution.py:229
  86.4 0.6 concatenate.22.table
  87.0 9.7 %collective-permute-done.4.after = bf16[720,128]{1,0:T(8,128)(2,1)S(1)} collective-permute-done((bf16[720,128]{1,0:T(8,128)(2,1)S(1)}, bf16[720,128]{1,0:T(8,128)(2,1)S(1)}, u32[]{:S(2)}, u32[]{:S(2)}) %collective-permute-start.4) | collective-permute-done | bytes 184352 | tf_op jit(solution)/shard_map/ppermute | solution.py:229
  96.7 9.8 %collective-permute-done.3.before = bf16[720,128]{1,0:T(8,128)(2,1)S(1)} collective-permute-done((bf16[720,128]{1,0:T(8,128)(2,1)S(1)}, bf16[720,128]{1,0:T(8,128)(2,1)S(1)}, u32[]{:S(2)}, u32[]{:S(2)}) %collective-permute-start.3) | collective-permute-done | bytes 184352 | tf_op jit(solution)/shard_map/ppermute | solution.py:229
  106.4 0.7 copy-done.15
  107.1 8.9 %short_range.1 = f32[256,512]{1,0:T(8,128)} custom-call(s32[2,13]{1,0:T(2,128)} %concatenate.22.table, bf16[720,128]{1,0:T(8,128)(2,1)} %copy-done.15, bf16[1328,128]{1,0:T(8,128)(2,1)} %copy-done.5, bf16[288,128]{1,0:T(8,128)(2,1)} %get-tuple-element.13.mine, bf16[1328,128]{1,0:T(8,128)(2,1)} %copy-done.6, bf16[720,128]{1,0:T(8,128)(2,1)} %copy-done.14, ...), custom_call_target="tpu_custom_call" | custom-call | flops 1100000000 | bytes 3000000 | tf_op jit(solution)/shard_map/short_range/pallas_call | solution.py:197
  116.0 0.6 convolution_convert_fusion
  116.6 0.6 fusion.3
  117.2 0.5 copy-done.1
  117.7 0.1 select_bitcast_fusion.1
  118.0 13.5 %all_to_all.15 = bf16[8,256,128]{2,1,0:T(8,128)(2,1)S(1)} all-to-all(bf16[8,256,128]{2,1,0:T(8,128)(2,1)S(1)} %bitcast.23), channel_id=1, replica_groups=mesh['z'=8,'xlo'=2,'y'=8,'xhi'=2,'core'=2] {'xlo','xhi','core'}, dimensions={0} | all-to-all | bytes 1048576 | tf_op jit(solution)/shard_map/all_to_all | solution.py:215
  131.5 0.7 reduce_sum.32
  (48 shorter events, 0.3 us)
Async XLA Ops:
  0.0 116.0 %copy-start = (bf16[256,512]{1,0:T(8,128)(2,1)S(1)}, bf16[256,512]{1,0:T(8,128)(2,1)}, u32[]{:S(2)}) copy-start(bf16[256,512]{1,0:T(8,128)(2,1)} %param.19) | copy-start | bytes 786436
  0.0 6.3 %copy-start.7 = (s32[3,256]{1,0:T(4,128)S(1)}, s32[3,256]{1,0:T(4,128)}, u32[]{:S(2)}) copy-start(s32[3,256]{1,0:T(4,128)} %positions.1) | copy-start | bytes 9220
  2.7 3.6 %copy-start.8 = (s32[3,1024]{1,0:T(4,128)S(1)}, s32[3,1024]{1,0:T(4,128)}, u32[]{:S(2)}) copy-start(s32[3,1024]{1,0:T(4,128)} %param.13) | copy-start | bytes 36868
  2.7 7.6 %collective-permute-start = (bf16[272,256]{1,0:T(8,128)(2,1)}, bf16[272,256]{1,0:T(8,128)(2,1)S(1)}, u32[]{:S(2)}, u32[]{:S(2)}) collective-permute-start(bf16[272,256]{1,0:T(8,128)(2,1)} %get-tuple-element.11), channel_id=1, source_target_pairs={{0,32},{1,33},{2,34},{3,35},{4,36},{5,37},{6,38},{7,39},{8,40},{9,... | collective-permute-start | bytes 417800 | tf_op jit(solution)/shard_map/ppermute | solution.py:229
  10.4 1.7 %copy-start.3 = (bf16[272,256]{1,0:T(8,128)(2,1)S(1)}, bf16[272,256]{1,0:T(8,128)(2,1)}, u32[]{:S(2)}) copy-start(bf16[272,256]{1,0:T(8,128)(2,1)} %get-tuple-element.11) | copy-start | bytes 417796
  13.6 34.6 %all-to-all-start = ((bf16[64,16,256]{2,1,0:T(8,128)(2,1)}), bf16[64,16,256]{2,1,0:T(8,128)(2,1)S(1)}, u32[]{:S(2)}, u32[]{:S(2)}) async-start(bf16[64,16,256]{2,1,0:T(8,128)(2,1)} %bitcast.10), calls=%async_computation | async-start | bytes 1048576 | tf_op jit(solution)/shard_map/all_to_all | solution.py:215
  30.2 18.1 %copy-start.2 = (f32[256,256]{1,0:T(8,128)S(1)}, f32[256,256]{1,0:T(8,128)}, u32[]{:S(2)}) copy-start(f32[256,256]{1,0:T(8,128)} %param.17) | copy-start | bytes 786436
  30.2 18.1 %copy-start.9 = (f32[256]{0:T(256)S(1)}, f32[256]{0:T(256)}, u32[]{:S(2)}) copy-start(f32[256]{0:T(256)} %param.18) | copy-start | bytes 3076
  49.3 5.9 %copy-start.12 = (bf16[1328,128]{1,0:T(8,128)(2,1)S(1)}, bf16[1328,128]{1,0:T(8,128)(2,1)}, u32[]{:S(2)}) copy-start(bf16[1328,128]{1,0:T(8,128)(2,1)} %get-tuple-element.12) | copy-start | bytes 1019908
  49.3 7.8 %copy-start.11 = (bf16[1328,128]{1,0:T(8,128)(2,1)S(1)}, bf16[1328,128]{1,0:T(8,128)(2,1)}, u32[]{:S(2)}) copy-start(bf16[1328,128]{1,0:T(8,128)(2,1)} %get-tuple-element.14) | copy-start | bytes 1019908
  49.3 14.0 %copy-start.13 = (bf16[1040,128]{1,0:T(8,128)(2,1)S(1)}, bf16[1040,128]{1,0:T(8,128)(2,1)}, u32[]{:S(2)}) copy-start(bf16[1040,128]{1,0:T(8,128)(2,1)} %get-tuple-element.16) | copy-start | bytes 798724
  49.3 66.7 %all-to-all-start.1 = ((bf16[64,16,256]{2,1,0:T(8,128)(2,1)}), bf16[64,16,256]{2,1,0:T(8,128)(2,1)S(1)}, u32[]{:S(2)}, u32[]{:S(2)}) async-start(bf16[64,16,256]{2,1,0:T(8,128)(2,1)} %broadcast_in_dim.2), calls=%async_computation.1 | async-start | bytes 1048576 | tf_op jit(solution)/shard_map/all_to_all | solution.py:215
  55.2 17.0 %collective-permute-start.1 = (bf16[1328,128]{1,0:T(8,128)(2,1)S(1)}, bf16[1328,128]{1,0:T(8,128)(2,1)S(1)}, u32[]{:S(2)}, u32[]{:S(2)}) collective-permute-start(bf16[1328,128]{1,0:T(8,128)(2,1)S(1)} %copy-done.12), channel_id=1, source_target_pairs={{0,5},{1,4},{2,7},{3,6},{4,9},{5,8},{6,11},{7,10},{8,13},{9,12},{1... | collective-permute-start | bytes 1019912 | tf_op jit(solution)/shard_map/ppermute | solution.py:229
  57.2 19.0 %collective-permute-start.2 = (bf16[1328,128]{1,0:T(8,128)(2,1)S(1)}, bf16[1328,128]{1,0:T(8,128)(2,1)S(1)}, u32[]{:S(2)}, u32[]{:S(2)}) collective-permute-start(bf16[1328,128]{1,0:T(8,128)(2,1)S(1)} %copy-done.11), channel_id=1, source_target_pairs={{0,511},{1,510},{2,509},{3,508},{4,3},{5,2},{6,1},{7,0},{8,7},{9,6... | collective-permute-start | bytes 1019912 | tf_op jit(solution)/shard_map/ppermute | solution.py:229
  63.3 23.7 %collective-permute-start.5 = (bf16[1040,128]{1,0:T(8,128)(2,1)S(1)}, bf16[1040,128]{1,0:T(8,128)(2,1)}, u32[]{:S(2)}, u32[]{:S(2)}) collective-permute-start(bf16[1040,128]{1,0:T(8,128)(2,1)S(1)} %copy-done.13), channel_id=1, source_target_pairs={{0,34},{1,35},{2,32},{3,33},{4,38},{5,39},{6,36},{7,37},{8,42},{9,... | collective-permute-start | bytes 798728 | tf_op jit(solution)/shard_map/ppermute | solution.py:229
  72.2 4.9 %copy-start.5 = (bf16[1328,128]{1,0:T(8,128)(2,1)}, bf16[1328,128]{1,0:T(8,128)(2,1)S(1)}, u32[]{:S(2)}) copy-start(bf16[1328,128]{1,0:T(8,128)(2,1)S(1)} %collective-permute-done.1.left) | copy-start | bytes 1019908
  76.2 1.0 copy-start.6
  76.2 1.0 copy-start.4
  77.2 9.2 %copy-start.10 = (s32[2,12]{1,0:T(2,128)S(1)}, s32[2,12]{1,0:T(2,128)}, u32[]{:S(2)}) copy-start(s32[2,12]{1,0:T(2,128)} %param.12) | copy-start | bytes 292
  77.2 19.5 %collective-permute-start.4 = (bf16[720,128]{1,0:T(8,128)(2,1)S(1)}, bf16[720,128]{1,0:T(8,128)(2,1)S(1)}, u32[]{:S(2)}, u32[]{:S(2)}) collective-permute-start(bf16[720,128]{1,0:T(8,128)(2,1)S(1)} %get-tuple-element.22), channel_id=1, source_target_pairs={{0,500},{1,501},{2,502},{3,503},{4,504},{5,505},{6,506},{7,507},{8... | collective-permute-start | bytes 552968 | tf_op jit(solution)/shard_map/ppermute | solution.py:229
  84.3 22.2 %collective-permute-start.3 = (bf16[720,128]{1,0:T(8,128)(2,1)S(1)}, bf16[720,128]{1,0:T(8,128)(2,1)S(1)}, u32[]{:S(2)}, u32[]{:S(2)}) collective-permute-start(bf16[720,128]{1,0:T(8,128)(2,1)S(1)} %get-tuple-element.23), channel_id=1, source_target_pairs={{0,12},{1,13},{2,14},{3,15},{4,16},{5,17},{6,18},{7,19},{8,20},{9,... | collective-permute-start | bytes 552968 | tf_op jit(solution)/shard_map/ppermute | solution.py:229
  96.7 9.8 %copy-start.14 = (bf16[720,128]{1,0:T(8,128)(2,1)}, bf16[720,128]{1,0:T(8,128)(2,1)S(1)}, u32[]{:S(2)}) copy-start(bf16[720,128]{1,0:T(8,128)(2,1)S(1)} %collective-permute-done.4.after) | copy-start | bytes 552964
  106.4 0.7 copy-start.15
  116.6 1.0 copy-start.1
